TPU v7x, 32 devices: a 4x4x1 block of a 4x4x8 slice. The times are simulated.
32 devices in a mesh: data: 1 (over z), model: 4 (over y), stage: 8 (over x, core).
Axes of the slice: x: 4, y: 4, z: 1, core: 2. Of those that a mesh axis runs over, the one named last changes fastest.
The devices are a block of a 4x4x8 slice.
Arguments:
- x_in: bfloat16 [1, 1024, 1536], P('data')
- y_target: bfloat16 [1, 1024, 1536], P('data')
- w_qkv: bfloat16 [8, 1536, 3, 12, 128], P('stage', None, None, 'model')
- w_out: bfloat16 [8, 12, 128, 1536], P('stage', 'model')
- w_up: bfloat16 [8, 1536, 6144], P('stage', None, 'model')
- w_down: bfloat16 [8, 6144, 1536], P('stage', 'model')
- norm_gain: bfloat16 [8, 2, 1536], P('stage')
Outputs:
- output 1: float32 [1], P('data')
- output 2: float32 [8, 1536, 3, 12, 128], P(('data', 'stage'), None, None, 'model')
- output 3: float32 [8, 12, 128, 1536], P(('data', 'stage'), 'model')
- output 4: float32 [8, 1536, 6144], P(('data', 'stage'), None, 'model')
- output 5: float32 [8, 6144, 1536], P(('data', 'stage'), 'model')
- output 6: float32 [8, 2, 1536], P(('data', 'stage'))
All inputs are finite; a program needn't handle non-finite values.
Results may differ from a plain program's by a relative error of at most 0.00889341.
Values are sent between devices in bfloat16 or wider.
A program may use at most 768 MiB of HBM per device.

v0:
```python
import jax
import jax.numpy as jnp
from jax import lax
from jax.sharding import PartitionSpec as P

NORM_EPS = 1e-6
NEG_BIG = -1e30


def rms_inverse(hid32):
    return lax.rsqrt(jnp.mean(hid32 * hid32, axis=-1, keepdims=True) + NORM_EPS)


def rms_backward(hid32, gain32, inv_rms, d_norm):
    normed = hid32 * inv_rms
    d_gain = jnp.sum(d_norm * normed, axis=(0, 1))
    d_normed = d_norm * gain32
    d_hid = inv_rms * (d_normed - normed * jnp.mean(d_normed * normed, axis=-1, keepdims=True))
    return d_hid, d_gain


def gelu_tanh(up_act):
    return jax.nn.gelu(up_act, approximate=True)


def causal_probs(q_blk, k_all, q_start, attn_scale):
    scores = jnp.einsum("bqhe,bkhe->bhqk", q_blk, k_all, preferred_element_type=jnp.float32) * attn_scale
    q_pos = q_start + jnp.arange(q_blk.shape[1])
    k_pos = jnp.arange(k_all.shape[1])
    scores = jnp.where(k_pos[None, :] <= q_pos[:, None], scores, NEG_BIG)
    return jax.nn.softmax(scores, axis=-1)


def attend_forward(q_blk, k_all, v_all, q_start, attn_scale):
    attn_probs = causal_probs(q_blk, k_all, q_start, attn_scale).astype(jnp.bfloat16)
    return jnp.einsum("bhqk,bkhe->bqhe", attn_probs, v_all, preferred_element_type=jnp.float32).astype(jnp.bfloat16)


def attend_backward(q_blk, k_all, v_all, d_attn, q_start, attn_scale):
    attn_probs = causal_probs(q_blk, k_all, q_start, attn_scale)
    d_probs = jnp.einsum("bqhe,bkhe->bhqk", d_attn, v_all, preferred_element_type=jnp.float32)
    d_scores = attn_probs * (d_probs - jnp.sum(attn_probs * d_probs, axis=-1, keepdims=True)) * attn_scale
    d_scores = d_scores.astype(jnp.bfloat16)
    d_q = jnp.einsum("bhqk,bkhe->bqhe", d_scores, k_all, preferred_element_type=jnp.float32)
    d_k = jnp.einsum("bhqk,bqhe->bkhe", d_scores, q_blk, preferred_element_type=jnp.float32)
    d_v = jnp.einsum("bhqk,bqhe->bkhe", attn_probs.astype(jnp.bfloat16), d_attn, preferred_element_type=jnp.float32)
    return d_q, d_k, d_v


def store_at(buf_all, new_val, index, is_valid):
    old_val = lax.dynamic_index_in_dim(buf_all, index, 0, keepdims=False)
    return lax.dynamic_update_index_in_dim(buf_all, jnp.where(is_valid, new_val, old_val), index, 0)


def load_at(buf_all, index):
    return lax.dynamic_index_in_dim(buf_all, index, 0, keepdims=False)


def solution(mesh):
    n_stage = mesh.shape["stage"]
    n_chunks = max(4, n_stage)
    n_ticks = n_chunks + n_stage - 1
    fwd_perm = [(src_dev, src_dev + 1) for src_dev in range(n_stage - 1)]
    bwd_perm = [(src_dev + 1, src_dev) for src_dev in range(n_stage - 1)]

    def device_fn(x_in, y_target, w_qkv, w_out, w_up, w_down, norm_gain):
        n_batch, seq_len, d_model = x_in.shape
        heads_loc = w_qkv.shape[3]
        head_dim = w_qkv.shape[4]
        ff_loc = w_up.shape[2]
        chunk_len = seq_len // n_chunks
        attn_scale = head_dim ** -0.5
        elem_count = n_batch * seq_len * d_model
        stage_idx = lax.axis_index("stage")
        is_first = stage_idx == 0
        is_last = stage_idx == n_stage - 1
        wqkv_loc = w_qkv[0]
        wout_loc = w_out[0]
        wup_loc = w_up[0]
        wdown_loc = w_down[0]
        gain_a = norm_gain[0, 0].astype(jnp.float32)
        gain_b = norm_gain[0, 1].astype(jnp.float32)
        act_shape = (n_batch, chunk_len, d_model)
        head_shape = (n_batch, chunk_len, heads_loc, head_dim)
        cache_shape = (n_batch, seq_len, heads_loc, head_dim)

        def put_rows(cache, new_rows, q_start, is_valid):
            old_rows = lax.dynamic_slice_in_dim(cache, q_start, chunk_len, 1)
            return lax.dynamic_update_slice_in_dim(cache, jnp.where(is_valid, new_rows, old_rows), q_start, 1)

        def layer_forward(h_in, q_start, is_valid, k_cache, v_cache):
            h32 = h_in.astype(jnp.float32)
            norm_a = (h32 * rms_inverse(h32) * gain_a).astype(jnp.bfloat16)
            qkv_act = jnp.einsum("btd,djhe->btjhe", norm_a, wqkv_loc, preferred_element_type=jnp.float32).astype(jnp.bfloat16)
            q_new = qkv_act[:, :, 0]
            k_cache = put_rows(k_cache, qkv_act[:, :, 1], q_start, is_valid)
            v_cache = put_rows(v_cache, qkv_act[:, :, 2], q_start, is_valid)
            attn_act = attend_forward(q_new, k_cache, v_cache, q_start, attn_scale)
            attn_part = jnp.einsum("bthe,hed->btd", attn_act, wout_loc, preferred_element_type=jnp.float32)
            mid_hid = h32 + lax.psum(attn_part, "model")
            norm_b = (mid_hid * rms_inverse(mid_hid) * gain_b).astype(jnp.bfloat16)
            up_act = jnp.einsum("btd,df->btf", norm_b, wup_loc, preferred_element_type=jnp.float32)
            gelu_act = gelu_tanh(up_act).astype(jnp.bfloat16)
            down_part = jnp.einsum("btf,fd->btd", gelu_act, wdown_loc, preferred_element_type=jnp.float32)
            h_out = (mid_hid + lax.psum(down_part, "model")).astype(jnp.bfloat16)
            return h_out, k_cache, v_cache, (h_in, mid_hid, q_new, attn_act, up_act)

        def fwd_tick(carry, tick_idx):
            recv_act, k_cache, v_cache, saved_bufs, out_grads, loss_sum = carry
            c_idx = tick_idx - stage_idx
            is_valid = (c_idx >= 0) & (c_idx < n_chunks)
            c_safe = jnp.clip(c_idx, 0, n_chunks - 1)
            q_start = c_safe * chunk_len
            x_rows = lax.dynamic_slice_in_dim(x_in, q_start, chunk_len, 1)
            h_in = jnp.where(is_first, x_rows, recv_act)
            h_out, k_cache, v_cache, saved = layer_forward(h_in, q_start, is_valid, k_cache, v_cache)
            saved_bufs = tuple(store_at(buf_all, new_val, c_safe, is_valid) for buf_all, new_val in zip(saved_bufs, saved))
            y_rows = lax.dynamic_slice_in_dim(y_target, q_start, chunk_len, 1)
            loss_diff = h_out.astype(jnp.float32) - y_rows.astype(jnp.float32)
            use_loss = is_valid & is_last
            loss_sum = loss_sum + jnp.where(use_loss, jnp.sum(loss_diff * loss_diff), 0.0)
            out_grads = store_at(out_grads, (loss_diff / elem_count).astype(jnp.bfloat16), c_safe, use_loss)
            recv_act = lax.ppermute(h_out, "stage", fwd_perm)
            return (recv_act, k_cache, v_cache, saved_bufs, out_grads, loss_sum), None

        saved_init = (
            jnp.zeros((n_chunks,) + act_shape, jnp.bfloat16),
            jnp.zeros((n_chunks,) + act_shape, jnp.float32),
            jnp.zeros((n_chunks,) + head_shape, jnp.bfloat16),
            jnp.zeros((n_chunks,) + head_shape, jnp.bfloat16),
            jnp.zeros((n_chunks, n_batch, chunk_len, ff_loc), jnp.float32),
        )
        fwd_init = (
            jnp.zeros(act_shape, jnp.bfloat16),
            jnp.zeros(cache_shape, jnp.bfloat16),
            jnp.zeros(cache_shape, jnp.bfloat16),
            saved_init,
            jnp.zeros((n_chunks,) + act_shape, jnp.bfloat16),
            jnp.zeros((), jnp.float32),
        )
        fwd_state = lax.scan(fwd_tick, fwd_init, jnp.arange(n_ticks))[0]
        k_cache = fwd_state[1]
        v_cache = fwd_state[2]
        saved_bufs = fwd_state[3]
        out_grads = fwd_state[4]
        loss_val = 0.5 * lax.psum(fwd_state[5], "stage") / elem_count

        def layer_backward(d_out, q_start, is_valid, saved, dk_acc, dv_acc):
            h_in, mid_hid, q_new, attn_act, up_act = saved
            h32 = h_in.astype(jnp.float32)
            inv_a = rms_inverse(h32)
            norm_a = (h32 * inv_a * gain_a).astype(jnp.bfloat16)
            inv_b = rms_inverse(mid_hid)
            norm_b = (mid_hid * inv_b * gain_b).astype(jnp.bfloat16)
            gelu_act, gelu_vjp = jax.vjp(gelu_tanh, up_act)
            grad_down = jnp.einsum("btf,btd->fd", gelu_act.astype(jnp.bfloat16), d_out, preferred_element_type=jnp.float32)
            d_gelu = jnp.einsum("btd,fd->btf", d_out, wdown_loc, preferred_element_type=jnp.float32)
            d_up = gelu_vjp(d_gelu)[0].astype(jnp.bfloat16)
            grad_up = jnp.einsum("btd,btf->df", norm_b, d_up, preferred_element_type=jnp.float32)
            d_norm_b = lax.psum(jnp.einsum("btf,df->btd", d_up, wup_loc, preferred_element_type=jnp.float32), "model")
            d_mid_norm, grad_gain_b = rms_backward(mid_hid, gain_b, inv_b, d_norm_b)
            d_mid = d_out.astype(jnp.float32) + d_mid_norm
            d_mid16 = d_mid.astype(jnp.bfloat16)
            grad_out = jnp.einsum("bthe,btd->hed", attn_act, d_mid16, preferred_element_type=jnp.float32)
            d_attn = jnp.einsum("btd,hed->bthe", d_mid16, wout_loc, preferred_element_type=jnp.float32).astype(jnp.bfloat16)
            d_q, d_k, d_v = attend_backward(q_new, k_cache, v_cache, d_attn, q_start, attn_scale)
            dk_acc = dk_acc + jnp.where(is_valid, d_k, 0.0)
            dv_acc = dv_acc + jnp.where(is_valid, d_v, 0.0)
            dk_rows = lax.dynamic_slice_in_dim(dk_acc, q_start, chunk_len, 1)
            dv_rows = lax.dynamic_slice_in_dim(dv_acc, q_start, chunk_len, 1)
            d_qkv = jnp.stack([d_q, dk_rows, dv_rows], axis=2).astype(jnp.bfloat16)
            grad_qkv = jnp.einsum("btd,btjhe->djhe", norm_a, d_qkv, preferred_element_type=jnp.float32)
            d_norm_a = lax.psum(jnp.einsum("btjhe,djhe->btd", d_qkv, wqkv_loc, preferred_element_type=jnp.float32), "model")
            d_h_norm, grad_gain_a = rms_backward(h32, gain_a, inv_a, d_norm_a)
            d_in = (d_mid + d_h_norm).astype(jnp.bfloat16)
            grad_new = (grad_qkv, grad_out, grad_up, grad_down, jnp.stack([grad_gain_a, grad_gain_b]))
            return d_in, dk_acc, dv_acc, grad_new

        def bwd_tick(carry, tick_idx):
            recv_grad, dk_acc, dv_acc, grad_sums = carry
            back_step = tick_idx - (n_stage - 1 - stage_idx)
            is_valid = (back_step >= 0) & (back_step < n_chunks)
            c_safe = jnp.clip(n_chunks - 1 - back_step, 0, n_chunks - 1)
            q_start = c_safe * chunk_len
            d_out = jnp.where(is_last, load_at(out_grads, c_safe), recv_grad)
            saved = tuple(load_at(buf_all, c_safe) for buf_all in saved_bufs)
            d_in, dk_acc, dv_acc, grad_new = layer_backward(d_out, q_start, is_valid, saved, dk_acc, dv_acc)
            grad_sums = tuple(grad_acc + jnp.where(is_valid, grad_part, 0.0) for grad_acc, grad_part in zip(grad_sums, grad_new))
            recv_grad = lax.ppermute(d_in, "stage", bwd_perm)
            return (recv_grad, dk_acc, dv_acc, grad_sums), None

        grad_init = (
            jnp.zeros(wqkv_loc.shape, jnp.float32),
            jnp.zeros(wout_loc.shape, jnp.float32),
            jnp.zeros(wup_loc.shape, jnp.float32),
            jnp.zeros(wdown_loc.shape, jnp.float32),
            jnp.zeros((2, d_model), jnp.float32),
        )
        bwd_init = (
            jnp.zeros(act_shape, jnp.bfloat16),
            jnp.zeros(cache_shape, jnp.float32),
            jnp.zeros(cache_shape, jnp.float32),
            grad_init,
        )
        grad_sums = lax.scan(bwd_tick, bwd_init, jnp.arange(n_ticks))[0][3]
        return (loss_val.reshape(1),) + tuple(grad_part[None] for grad_part in grad_sums)

    act_spec = P("data", None, None)
    weight_specs = (
        P("stage", None, None, "model", None),
        P("stage", "model", None, None),
        P("stage", None, "model"),
        P("stage", "model", None),
        P("stage", None, None),
    )
    grad_specs = (
        P(("data", "stage"), None, None, "model", None),
        P(("data", "stage"), "model", None, None),
        P(("data", "stage"), None, "model"),
        P(("data", "stage"), "model", None),
        P(("data", "stage"), None, None),
    )
    return jax.shard_map(
        device_fn,
        mesh=mesh,
        in_specs=(act_spec, act_spec) + weight_specs,
        out_specs=(P("data"),) + grad_specs,
        check_vma=False,
    )
```

profile of v0, /device:TPU:96, one launch (start us, length us, event | category | flops | bytes accessed | tf_op | source)
XLA Modules:
  0.0 3726.0 jit_solution(11255984542755003397)
XLA Ops:
  28.1 1743.7 %while.55 = (s32[]{:T(128)}, bf16[1,128,1536]{2,1,0:T(8,128)(2,1)S(1)}, bf16[1,1024,3,128]{3,1,2,0:T(8,128)(2,1)}, bf16[1,1024,3,128]{3,1,2,0:T(8,128)(2,1)}, bf...) while((s32[]{:T(128)}, ...), condition=%wide.region_8.9_spmd, body=%wide.region_0.8_spmd.sunk | while | flops 2025588096 | bytes 70964376 | solution.py:141
  49.3 38.6 %all-reduce.5.cloned.1.call-done = f32[1,128,1536]{2,1,0:T(8,128)} async-done(((f32[1,128,1536]{2,1,0:T(8,128)}), f32[1,128,1536]{2,1,0:T(8,128)}) %all-reduce.5.cloned.1.call-update) | async-done | bytes 786448 | tf_op jit(solution)/shard_map/while/body/eval_jaxpr/psum | solution.py:100
  97.9 37.7 %all-reduce.7.cloned.1.call-done = f32[1,128,1536]{2,1,0:T(8,128)} async-done(((f32[1,128,1536]{2,1,0:T(8,128)}), f32[1,128,1536]{2,1,0:T(8,128)}) %all-reduce.7.cloned.1.call-update) | async-done | bytes 786448 | tf_op jit(solution)/shard_map/while/body/eval_jaxpr/psum | solution.py:105
  162.9 41.4 %all-reduce.5.cloned.1.call-done = f32[1,128,1536]{2,1,0:T(8,128)} async-done(((f32[1,128,1536]{2,1,0:T(8,128)}), f32[1,128,1536]{2,1,0:T(8,128)}) %all-reduce.5.cloned.1.call-update) | async-done | bytes 786448 | tf_op jit(solution)/shard_map/while/body/eval_jaxpr/psum | solution.py:100
  214.3 37.8 %all-reduce.7.cloned.1.call-done = f32[1,128,1536]{2,1,0:T(8,128)} async-done(((f32[1,128,1536]{2,1,0:T(8,128)}), f32[1,128,1536]{2,1,0:T(8,128)}) %all-reduce.7.cloned.1.call-update) | async-done | bytes 786448 | tf_op jit(solution)/shard_map/while/body/eval_jaxpr/psum | solution.py:105
  279.3 41.5 %all-reduce.5.cloned.1.call-done = f32[1,128,1536]{2,1,0:T(8,128)} async-done(((f32[1,128,1536]{2,1,0:T(8,128)}), f32[1,128,1536]{2,1,0:T(8,128)}) %all-reduce.5.cloned.1.call-update) | async-done | bytes 786448 | tf_op jit(solution)/shard_map/while/body/eval_jaxpr/psum | solution.py:100
  330.8 37.7 %all-reduce.7.cloned.1.call-done = f32[1,128,1536]{2,1,0:T(8,128)} async-done(((f32[1,128,1536]{2,1,0:T(8,128)}), f32[1,128,1536]{2,1,0:T(8,128)}) %all-reduce.7.cloned.1.call-update) | async-done | bytes 786448 | tf_op jit(solution)/shard_map/while/body/eval_jaxpr/psum | solution.py:105
  395.7 41.4 %all-reduce.5.cloned.1.call-done = f32[1,128,1536]{2,1,0:T(8,128)} async-done(((f32[1,128,1536]{2,1,0:T(8,128)}), f32[1,128,1536]{2,1,0:T(8,128)}) %all-reduce.5.cloned.1.call-update) | async-done | bytes 786448 | tf_op jit(solution)/shard_map/while/body/eval_jaxpr/psum | solution.py:100
  447.3 37.6 %all-reduce.7.cloned.1.call-done = f32[1,128,1536]{2,1,0:T(8,128)} async-done(((f32[1,128,1536]{2,1,0:T(8,128)}), f32[1,128,1536]{2,1,0:T(8,128)}) %all-reduce.7.cloned.1.call-update) | async-done | bytes 786448 | tf_op jit(solution)/shard_map/while/body/eval_jaxpr/psum | solution.py:105
  512.1 41.5 %all-reduce.5.cloned.1.call-done = f32[1,128,1536]{2,1,0:T(8,128)} async-done(((f32[1,128,1536]{2,1,0:T(8,128)}), f32[1,128,1536]{2,1,0:T(8,128)}) %all-reduce.5.cloned.1.call-update) | async-done | bytes 786448 | tf_op jit(solution)/shard_map/while/body/eval_jaxpr/psum | solution.py:100
  563.6 37.7 %all-reduce.7.cloned.1.call-done = f32[1,128,1536]{2,1,0:T(8,128)} async-done(((f32[1,128,1536]{2,1,0:T(8,128)}), f32[1,128,1536]{2,1,0:T(8,128)}) %all-reduce.7.cloned.1.call-update) | async-done | bytes 786448 | tf_op jit(solution)/shard_map/while/body/eval_jaxpr/psum | solution.py:105
  628.5 41.5 %all-reduce.5.cloned.1.call-done = f32[1,128,1536]{2,1,0:T(8,128)} async-done(((f32[1,128,1536]{2,1,0:T(8,128)}), f32[1,128,1536]{2,1,0:T(8,128)}) %all-reduce.5.cloned.1.call-update) | async-done | bytes 786448 | tf_op jit(solution)/shard_map/while/body/eval_jaxpr/psum | solution.py:100
  680.0 37.7 %all-reduce.7.cloned.1.call-done = f32[1,128,1536]{2,1,0:T(8,128)} async-done(((f32[1,128,1536]{2,1,0:T(8,128)}), f32[1,128,1536]{2,1,0:T(8,128)}) %all-reduce.7.cloned.1.call-update) | async-done | bytes 786448 | tf_op jit(solution)/shard_map/while/body/eval_jaxpr/psum | solution.py:105
  745.0 41.4 %all-reduce.5.cloned.1.call-done = f32[1,128,1536]{2,1,0:T(8,128)} async-done(((f32[1,128,1536]{2,1,0:T(8,128)}), f32[1,128,1536]{2,1,0:T(8,128)}) %all-reduce.5.cloned.1.call-update) | async-done | bytes 786448 | tf_op jit(solution)/shard_map/while/body/eval_jaxpr/psum | solution.py:100
  796.4 37.8 %all-reduce.7.cloned.1.call-done = f32[1,128,1536]{2,1,0:T(8,128)} async-done(((f32[1,128,1536]{2,1,0:T(8,128)}), f32[1,128,1536]{2,1,0:T(8,128)}) %all-reduce.7.cloned.1.call-update) | async-done | bytes 786448 | tf_op jit(solution)/shard_map/while/body/eval_jaxpr/psum | solution.py:105
  861.5 41.4 %all-reduce.5.cloned.1.call-done = f32[1,128,1536]{2,1,0:T(8,128)} async-done(((f32[1,128,1536]{2,1,0:T(8,128)}), f32[1,128,1536]{2,1,0:T(8,128)}) %all-reduce.5.cloned.1.call-update) | async-done | bytes 786448 | tf_op jit(solution)/shard_map/while/body/eval_jaxpr/psum | solution.py:100
  913.0 37.8 %all-reduce.7.cloned.1.call-done = f32[1,128,1536]{2,1,0:T(8,128)} async-done(((f32[1,128,1536]{2,1,0:T(8,128)}), f32[1,128,1536]{2,1,0:T(8,128)}) %all-reduce.7.cloned.1.call-update) | async-done | bytes 786448 | tf_op jit(solution)/shard_map/while/body/eval_jaxpr/psum | solution.py:105
  977.9 41.4 %all-reduce.5.cloned.1.call-done = f32[1,128,1536]{2,1,0:T(8,128)} async-done(((f32[1,128,1536]{2,1,0:T(8,128)}), f32[1,128,1536]{2,1,0:T(8,128)}) %all-reduce.5.cloned.1.call-update) | async-done | bytes 786448 | tf_op jit(solution)/shard_map/while/body/eval_jaxpr/psum | solution.py:100
  1029.4 37.7 %all-reduce.7.cloned.1.call-done = f32[1,128,1536]{2,1,0:T(8,128)} async-done(((f32[1,128,1536]{2,1,0:T(8,128)}), f32[1,128,1536]{2,1,0:T(8,128)}) %all-reduce.7.cloned.1.call-update) | async-done | bytes 786448 | tf_op jit(solution)/shard_map/while/body/eval_jaxpr/psum | solution.py:105
  1094.3 41.5 %all-reduce.5.cloned.1.call-done = f32[1,128,1536]{2,1,0:T(8,128)} async-done(((f32[1,128,1536]{2,1,0:T(8,128)}), f32[1,128,1536]{2,1,0:T(8,128)}) %all-reduce.5.cloned.1.call-update) | async-done | bytes 786448 | tf_op jit(solution)/shard_map/while/body/eval_jaxpr/psum | solution.py:100
  1145.9 37.7 %all-reduce.7.cloned.1.call-done = f32[1,128,1536]{2,1,0:T(8,128)} async-done(((f32[1,128,1536]{2,1,0:T(8,128)}), f32[1,128,1536]{2,1,0:T(8,128)}) %all-reduce.7.cloned.1.call-update) | async-done | bytes 786448 | tf_op jit(solution)/shard_map/while/body/eval_jaxpr/psum | solution.py:105
  1210.9 41.4 %all-reduce.5.cloned.1.call-done = f32[1,128,1536]{2,1,0:T(8,128)} async-done(((f32[1,128,1536]{2,1,0:T(8,128)}), f32[1,128,1536]{2,1,0:T(8,128)}) %all-reduce.5.cloned.1.call-update) | async-done | bytes 786448 | tf_op jit(solution)/shard_map/while/body/eval_jaxpr/psum | solution.py:100
  1262.3 37.7 %all-reduce.7.cloned.1.call-done = f32[1,128,1536]{2,1,0:T(8,128)} async-done(((f32[1,128,1536]{2,1,0:T(8,128)}), f32[1,128,1536]{2,1,0:T(8,128)}) %all-reduce.7.cloned.1.call-update) | async-done | bytes 786448 | tf_op jit(solution)/shard_map/while/body/eval_jaxpr/psum | solution.py:105
  1327.3 41.4 %all-reduce.5.cloned.1.call-done = f32[1,128,1536]{2,1,0:T(8,128)} async-done(((f32[1,128,1536]{2,1,0:T(8,128)}), f32[1,128,1536]{2,1,0:T(8,128)}) %all-reduce.5.cloned.1.call-update) | async-done | bytes 786448 | tf_op jit(solution)/shard_map/while/body/eval_jaxpr/psum | solution.py:100
  1378.8 37.8 %all-reduce.7.cloned.1.call-done = f32[1,128,1536]{2,1,0:T(8,128)} async-done(((f32[1,128,1536]{2,1,0:T(8,128)}), f32[1,128,1536]{2,1,0:T(8,128)}) %all-reduce.7.cloned.1.call-update) | async-done | bytes 786448 | tf_op jit(solution)/shard_map/while/body/eval_jaxpr/psum | solution.py:105
  1443.8 41.4 %all-reduce.5.cloned.1.call-done = f32[1,128,1536]{2,1,0:T(8,128)} async-done(((f32[1,128,1536]{2,1,0:T(8,128)}), f32[1,128,1536]{2,1,0:T(8,128)}) %all-reduce.5.cloned.1.call-update) | async-done | bytes 786448 | tf_op jit(solution)/shard_map/while/body/eval_jaxpr/psum | solution.py:100
  1495.3 37.7 %all-reduce.7.cloned.1.call-done = f32[1,128,1536]{2,1,0:T(8,128)} async-done(((f32[1,128,1536]{2,1,0:T(8,128)}), f32[1,128,1536]{2,1,0:T(8,128)}) %all-reduce.7.cloned.1.call-update) | async-done | bytes 786448 | tf_op jit(solution)/shard_map/while/body/eval_jaxpr/psum | solution.py:105
  1560.2 41.4 %all-reduce.5.cloned.1.call-done = f32[1,128,1536]{2,1,0:T(8,128)} async-done(((f32[1,128,1536]{2,1,0:T(8,128)}), f32[1,128,1536]{2,1,0:T(8,128)}) %all-reduce.5.cloned.1.call-update) | async-done | bytes 786448 | tf_op jit(solution)/shard_map/while/body/eval_jaxpr/psum | solution.py:100
  1611.7 37.7 %all-reduce.7.cloned.1.call-done = f32[1,128,1536]{2,1,0:T(8,128)} async-done(((f32[1,128,1536]{2,1,0:T(8,128)}), f32[1,128,1536]{2,1,0:T(8,128)}) %all-reduce.7.cloned.1.call-update) | async-done | bytes 786448 | tf_op jit(solution)/shard_map/while/body/eval_jaxpr/psum | solution.py:105
  1676.6 41.5 %all-reduce.5.cloned.1.call-done = f32[1,128,1536]{2,1,0:T(8,128)} async-done(((f32[1,128,1536]{2,1,0:T(8,128)}), f32[1,128,1536]{2,1,0:T(8,128)}) %all-reduce.5.cloned.1.call-update) | async-done | bytes 786448 | tf_op jit(solution)/shard_map/while/body/eval_jaxpr/psum | solution.py:100
  1728.1 37.7 %all-reduce.7.cloned.1.call-done = f32[1,128,1536]{2,1,0:T(8,128)} async-done(((f32[1,128,1536]{2,1,0:T(8,128)}), f32[1,128,1536]{2,1,0:T(8,128)}) %all-reduce.7.cloned.1.call-update) | async-done | bytes 786448 | tf_op jit(solution)/shard_map/while/body/eval_jaxpr/psum | solution.py:105
  1790.7 1927.3 %while.56 = (s32[]{:T(128)}, bf16[1,128,1536]{2,1,0:T(8,128)(2,1)S(1)}, f32[1,1024,3,128]{3,1,2,0:T(8,128)}, f32[1,1024,3,128]{3,1,2,0:T(8,128)}, f32[1536,3,3,1...) while((s32[]{:T(128)}, ...), condition=%wide.region_22.23_spmd.clone, body=%wide.region_10.22_spmd.clone.sunk | while | flops 4174623744 | bytes 145293552 | solution.py:205
  1872.9 32.1 all-reduce.11.cloned.1.call-done
  2004.9 29.1 all-reduce.11.cloned.1.call-done
  2133.9 29.1 all-reduce.11.cloned.1.call-done
  2262.9 29.1 all-reduce.11.cloned.1.call-done
  2391.9 29.2 all-reduce.11.cloned.1.call-done
  2520.9 29.2 all-reduce.11.cloned.1.call-done
  2649.9 29.1 all-reduce.11.cloned.1.call-done
  2720.1 20.6 all-reduce.9.cloned.1.call-done
  2779.0 29.1 all-reduce.11.cloned.1.call-done
  2907.9 29.1 all-reduce.11.cloned.1.call-done
  3036.9 29.2 all-reduce.11.cloned.1.call-done
  3166.0 29.1 all-reduce.11.cloned.1.call-done
  3295.0 29.2 all-reduce.11.cloned.1.call-done
  3424.0 29.2 all-reduce.11.cloned.1.call-done
  3553.1 29.2 all-reduce.11.cloned.1.call-done
  3682.1 29.2 all-reduce.11.cloned.1.call-done
  (1313 shorter events, 2031.6 us)
Async XLA Ops:
  28.1 59.8 %all-reduce.5.cloned.1.call-start = ((), (), s32[]{:S(2)}) async-start(), calls=%async_computation | async-start | bytes 1572864 | tf_op jit(solution)/shard_map/while/body/eval_jaxpr/psum | solution.py:100
  45.5 90.2 %all-reduce.7.cloned.1.call-start = ((), (), s32[]{:S(2)}) async-start(), calls=%async_computation.1 | async-start | bytes 1572864 | tf_op jit(solution)/shard_map/while/body/eval_jaxpr/psum | solution.py:105
  141.6 62.7 %all-reduce.5.cloned.1.call-start = ((), (), s32[]{:S(2)}) async-start(), calls=%async_computation | async-start | bytes 1572864 | tf_op jit(solution)/shard_map/while/body/eval_jaxpr/psum | solution.py:100
  159.0 93.1 %all-reduce.7.cloned.1.call-start = ((), (), s32[]{:S(2)}) async-start(), calls=%async_computation.1 | async-start | bytes 1572864 | tf_op jit(solution)/shard_map/while/body/eval_jaxpr/psum | solution.py:105
  258.0 62.7 %all-reduce.5.cloned.1.call-start = ((), (), s32[]{:S(2)}) async-start(), calls=%async_computation | async-start | bytes 1572864 | tf_op jit(solution)/shard_map/while/body/eval_jaxpr/psum | solution.py:100
  275.4 93.1 %all-reduce.7.cloned.1.call-start = ((), (), s32[]{:S(2)}) async-start(), calls=%async_computation.1 | async-start | bytes 1572864 | tf_op jit(solution)/shard_map/while/body/eval_jaxpr/psum | solution.py:105
  374.5 62.7 %all-reduce.5.cloned.1.call-start = ((), (), s32[]{:S(2)}) async-start(), calls=%async_computation | async-start | bytes 1572864 | tf_op jit(solution)/shard_map/while/body/eval_jaxpr/psum | solution.py:100
  391.9 93.0 %all-reduce.7.cloned.1.call-start = ((), (), s32[]{:S(2)}) async-start(), calls=%async_computation.1 | async-start | bytes 1572864 | tf_op jit(solution)/shard_map/while/body/eval_jaxpr/psum | solution.py:105
  490.9 62.7 %all-reduce.5.cloned.1.call-start = ((), (), s32[]{:S(2)}) async-start(), calls=%async_computation | async-start | bytes 1572864 | tf_op jit(solution)/shard_map/while/body/eval_jaxpr/psum | solution.py:100
  508.3 93.1 %all-reduce.7.cloned.1.call-start = ((), (), s32[]{:S(2)}) async-start(), calls=%async_computation.1 | async-start | bytes 1572864 | tf_op jit(solution)/shard_map/while/body/eval_jaxpr/psum | solution.py:105
  607.3 62.7 %all-reduce.5.cloned.1.call-start = ((), (), s32[]{:S(2)}) async-start(), calls=%async_computation | async-start | bytes 1572864 | tf_op jit(solution)/shard_map/while/body/eval_jaxpr/psum | solution.py:100
  624.7 93.1 %all-reduce.7.cloned.1.call-start = ((), (), s32[]{:S(2)}) async-start(), calls=%async_computation.1 | async-start | bytes 1572864 | tf_op jit(solution)/shard_map/while/body/eval_jaxpr/psum | solution.py:105
  723.7 62.7 %all-reduce.5.cloned.1.call-start = ((), (), s32[]{:S(2)}) async-start(), calls=%async_computation | async-start | bytes 1572864 | tf_op jit(solution)/shard_map/while/body/eval_jaxpr/psum | solution.py:100
  741.1 93.1 %all-reduce.7.cloned.1.call-start = ((), (), s32[]{:S(2)}) async-start(), calls=%async_computation.1 | async-start | bytes 1572864 | tf_op jit(solution)/shard_map/while/body/eval_jaxpr/psum | solution.py:105
  840.2 62.7 %all-reduce.5.cloned.1.call-start = ((), (), s32[]{:S(2)}) async-start(), calls=%async_computation | async-start | bytes 1572864 | tf_op jit(solution)/shard_map/while/body/eval_jaxpr/psum | solution.py:100
  857.6 93.1 %all-reduce.7.cloned.1.call-start = ((), (), s32[]{:S(2)}) async-start(), calls=%async_computation.1 | async-start | bytes 1572864 | tf_op jit(solution)/shard_map/while/body/eval_jaxpr/psum | solution.py:105
  956.7 62.7 %all-reduce.5.cloned.1.call-start = ((), (), s32[]{:S(2)}) async-start(), calls=%async_computation | async-start | bytes 1572864 | tf_op jit(solution)/shard_map/while/body/eval_jaxpr/psum | solution.py:100
  974.1 93.1 %all-reduce.7.cloned.1.call-start = ((), (), s32[]{:S(2)}) async-start(), calls=%async_computation.1 | async-start | bytes 1572864 | tf_op jit(solution)/shard_map/while/body/eval_jaxpr/psum | solution.py:105
  1073.1 62.7 %all-reduce.5.cloned.1.call-start = ((), (), s32[]{:S(2)}) async-start(), calls=%async_computation | async-start | bytes 1572864 | tf_op jit(solution)/shard_map/while/body/eval_jaxpr/psum | solution.py:100
  1090.5 93.1 %all-reduce.7.cloned.1.call-start = ((), (), s32[]{:S(2)}) async-start(), calls=%async_computation.1 | async-start | bytes 1572864 | tf_op jit(solution)/shard_map/while/body/eval_jaxpr/psum | solution.py:105
  1189.6 62.7 %all-reduce.5.cloned.1.call-start = ((), (), s32[]{:S(2)}) async-start(), calls=%async_computation | async-start | bytes 1572864 | tf_op jit(solution)/shard_map/while/body/eval_jaxpr/psum | solution.py:100
  1207.0 93.1 %all-reduce.7.cloned.1.call-start = ((), (), s32[]{:S(2)}) async-start(), calls=%async_computation.1 | async-start | bytes 1572864 | tf_op jit(solution)/shard_map/while/body/eval_jaxpr/psum | solution.py:105
  1306.0 62.7 %all-reduce.5.cloned.1.call-start = ((), (), s32[]{:S(2)}) async-start(), calls=%async_computation | async-start | bytes 1572864 | tf_op jit(solution)/shard_map/while/body/eval_jaxpr/psum | solution.py:100
  1323.4 93.1 %all-reduce.7.cloned.1.call-start = ((), (), s32[]{:S(2)}) async-start(), calls=%async_computation.1 | async-start | bytes 1572864 | tf_op jit(solution)/shard_map/while/body/eval_jaxpr/psum | solution.py:105
  1422.5 62.7 %all-reduce.5.cloned.1.call-start = ((), (), s32[]{:S(2)}) async-start(), calls=%async_computation | async-start | bytes 1572864 | tf_op jit(solution)/shard_map/while/body/eval_jaxpr/psum | solution.py:100
  1439.9 93.1 %all-reduce.7.cloned.1.call-start = ((), (), s32[]{:S(2)}) async-start(), calls=%async_computation.1 | async-start | bytes 1572864 | tf_op jit(solution)/shard_map/while/body/eval_jaxpr/psum | solution.py:105
  1538.9 62.7 %all-reduce.5.cloned.1.call-start = ((), (), s32[]{:S(2)}) async-start(), calls=%async_computation | async-start | bytes 1572864 | tf_op jit(solution)/shard_map/while/body/eval_jaxpr/psum | solution.py:100
  1556.3 93.1 %all-reduce.7.cloned.1.call-start = ((), (), s32[]{:S(2)}) async-start(), calls=%async_computation.1 | async-start | bytes 1572864 | tf_op jit(solution)/shard_map/while/body/eval_jaxpr/psum | solution.py:105
  1655.4 62.7 %all-reduce.5.cloned.1.call-start = ((), (), s32[]{:S(2)}) async-start(), calls=%async_computation | async-start | bytes 1572864 | tf_op jit(solution)/shard_map/while/body/eval_jaxpr/psum | solution.py:100
  1672.7 93.1 %all-reduce.7.cloned.1.call-start = ((), (), s32[]{:S(2)}) async-start(), calls=%async_computation.1 | async-start | bytes 1572864 | tf_op jit(solution)/shard_map/while/body/eval_jaxpr/psum | solution.py:105
  1801.1 104.0 %all-reduce.11.cloned.1.call-start = ((), (), s32[]{:S(2)}) async-start(), calls=%async_computation.3 | async-start | bytes 1572864 | tf_op jit(solution)/shard_map/while/body/eval_jaxpr/psum | solution.py:173
  1921.9 112.1 %all-reduce.11.cloned.1.call-start = ((), (), s32[]{:S(2)}) async-start(), calls=%async_computation.3 | async-start | bytes 1572864 | tf_op jit(solution)/shard_map/while/body/eval_jaxpr/psum | solution.py:173
  2051.0 112.1 %all-reduce.11.cloned.1.call-start = ((), (), s32[]{:S(2)}) async-start(), calls=%async_computation.3 | async-start | bytes 1572864 | tf_op jit(solution)/shard_map/while/body/eval_jaxpr/psum | solution.py:173
  2179.9 112.1 %all-reduce.11.cloned.1.call-start = ((), (), s32[]{:S(2)}) async-start(), calls=%async_computation.3 | async-start | bytes 1572864 | tf_op jit(solution)/shard_map/while/body/eval_jaxpr/psum | solution.py:173
  2308.9 112.1 %all-reduce.11.cloned.1.call-start = ((), (), s32[]{:S(2)}) async-start(), calls=%async_computation.3 | async-start | bytes 1572864 | tf_op jit(solution)/shard_map/while/body/eval_jaxpr/psum | solution.py:173
  2427.8 54.9 %all-reduce.9.cloned.1.call-start = ((), (), s32[]{:S(2)}) async-start(), calls=%async_computation.2 | async-start | bytes 1572864 | tf_op jit(solution)/shard_map/while/body/eval_jaxpr/psum | solution.py:160
  2437.9 112.2 %all-reduce.11.cloned.1.call-start = ((), (), s32[]{:S(2)}) async-start(), calls=%async_computation.3 | async-start | bytes 1572864 | tf_op jit(solution)/shard_map/while/body/eval_jaxpr/psum | solution.py:173
  2567.0 112.1 %all-reduce.11.cloned.1.call-start = ((), (), s32[]{:S(2)}) async-start(), calls=%async_computation.3 | async-start | bytes 1572864 | tf_op jit(solution)/shard_map/while/body/eval_jaxpr/psum | solution.py:173
  2685.8 54.9 %all-reduce.9.cloned.1.call-start = ((), (), s32[]{:S(2)}) async-start(), calls=%async_computation.2 | async-start | bytes 1572864 | tf_op jit(solution)/shard_map/while/body/eval_jaxpr/psum | solution.py:160
  2696.0 112.1 %all-reduce.11.cloned.1.call-start = ((), (), s32[]{:S(2)}) async-start(), calls=%async_computation.3 | async-start | bytes 1572864 | tf_op jit(solution)/shard_map/while/body/eval_jaxpr/psum | solution.py:173
  2824.9 112.1 %all-reduce.11.cloned.1.call-start = ((), (), s32[]{:S(2)}) async-start(), calls=%async_computation.3 | async-start | bytes 1572864 | tf_op jit(solution)/shard_map/while/body/eval_jaxpr/psum | solution.py:173
  2943.8 54.9 %all-reduce.9.cloned.1.call-start = ((), (), s32[]{:S(2)}) async-start(), calls=%async_computation.2 | async-start | bytes 1572864 | tf_op jit(solution)/shard_map/while/body/eval_jaxpr/psum | solution.py:160
  2953.9 112.1 %all-reduce.11.cloned.1.call-start = ((), (), s32[]{:S(2)}) async-start(), calls=%async_computation.3 | async-start | bytes 1572864 | tf_op jit(solution)/shard_map/while/body/eval_jaxpr/psum | solution.py:173
  3083.0 112.1 %all-reduce.11.cloned.1.call-start = ((), (), s32[]{:S(2)}) async-start(), calls=%async_computation.3 | async-start | bytes 1572864 | tf_op jit(solution)/shard_map/while/body/eval_jaxpr/psum | solution.py:173
  3212.0 112.1 %all-reduce.11.cloned.1.call-start = ((), (), s32[]{:S(2)}) async-start(), calls=%async_computation.3 | async-start | bytes 1572864 | tf_op jit(solution)/shard_map/while/body/eval_jaxpr/psum | solution.py:173
  3341.0 112.1 %all-reduce.11.cloned.1.call-start = ((), (), s32[]{:S(2)}) async-start(), calls=%async_computation.3 | async-start | bytes 1572864 | tf_op jit(solution)/shard_map/while/body/eval_jaxpr/psum | solution.py:173
  3470.1 112.1 %all-reduce.11.cloned.1.call-start = ((), (), s32[]{:S(2)}) async-start(), calls=%async_computation.3 | async-start | bytes 1572864 | tf_op jit(solution)/shard_map/while/body/eval_jaxpr/psum | solution.py:173
  3599.1 112.1 %all-reduce.11.cloned.1.call-start = ((), (), s32[]{:S(2)}) async-start(), calls=%async_computation.3 | async-start | bytes 1572864 | tf_op jit(solution)/shard_map/while/body/eval_jaxpr/psum | solution.py:173
  (163 other events, 1685.8 us)
Sparse Core Ops, SparseCore 0:
  45.6 42.2 all-reduce.4
  159.1 45.0 all-reduce.4
  212.1 39.9 all-reduce.6
  275.6 45.1 all-reduce.4
  392.0 45.1 all-reduce.4
  508.4 45.1 all-reduce.4
  624.8 45.1 all-reduce.4
  741.2 45.1 all-reduce.4
  794.2 39.9 all-reduce.6
  857.7 45.0 all-reduce.4
  910.7 39.9 all-reduce.6
  974.2 45.1 all-reduce.4
  1027.1 39.9 all-reduce.6
  1090.6 45.1 all-reduce.4
  1143.6 39.9 all-reduce.6
  1207.1 45.1 all-reduce.4
  1260.1 39.9 all-reduce.6
  1323.6 45.1 all-reduce.4
  1376.5 39.9 all-reduce.6
  1440.0 45.1 all-reduce.4
  1556.4 45.1 all-reduce.4
  1609.4 39.9 all-reduce.6
  1672.9 45.1 all-reduce.4
  1865.1 39.9 all-reduce.10
  1922.1 44.6 all-reduce.8
  2051.1 44.5 all-reduce.8
  2180.1 44.5 all-reduce.8
  2309.0 44.5 all-reduce.8
  2381.1 39.9 all-reduce.10
  2438.1 44.6 all-reduce.8
  2510.1 39.9 all-reduce.10
  2567.1 44.5 all-reduce.8
  2639.1 39.9 all-reduce.10
  2696.1 44.6 all-reduce.8
  2825.1 44.5 all-reduce.8
  2897.1 39.9 all-reduce.10
  2954.1 44.6 all-reduce.8
  3026.1 39.9 all-reduce.10
  3083.1 44.6 all-reduce.8
  3155.2 39.9 all-reduce.10
  3212.1 44.6 all-reduce.8
  3284.1 39.9 all-reduce.10
  3341.2 44.6 all-reduce.8
  3413.2 39.9 all-reduce.10
  3470.2 44.6 all-reduce.8
  3542.2 39.9 all-reduce.10
  3599.2 44.6 all-reduce.8
  3671.3 39.9 all-reduce.10
  (12 shorter events, 476.4 us)
where the time goes:
time: 3750 us; the launch traced here: 3730 us
  waiting for transfers between devices  1970 us (53%)
  matrix products  1160 us (31%)
  other arithmetic  334 us (9%)
  local copies, waits for them, and re-layouts  154 us (4%)
  starting transfers between devices  41.4 us (1%)
    psum x15, waiting for transfers between devices, layer_forward(): mid_hid = h32 + lax.psum(attn_part, 'model')  619 us
    psum x15, waiting for transfers between devices, layer_forward(): h_out = (mid_hid + lax.psum(down_part, 'model')).astype(jnp.bfloat16)  566 us
    psum x15, waiting for transfers between devices, layer_backward(): lax.psum(jnp.einsum('btjhe,djhe->btd', d_qkv, wqkv_loc, preferred_element...  440 us
    psum x15, waiting for transfers between devices, layer_backward(): lax.psum(jnp.einsum('btf,df->btd', d_up, wup_loc, preferred_element_type=...  309 us
    dot_general x15, matrix products, layer_backward(): jnp.einsum('btf,btd->fd', gelu_act.astype(jnp.bfloat16), d_out, preferred...  135 us
    dot_general x15, matrix products, layer_backward(): jnp.einsum('btd,btf->df', norm_b, d_up, preferred_element_type=jnp.float32)  135 us
    dot_general x15, matrix products, attend_backward(): jnp.einsum('bhqk,bqhe->bkhe', d_scores, q_blk, preferred_element_type=jnp...  109 us
    dot_general x15, matrix products, layer_backward(): jnp.einsum('btd,btjhe->djhe', norm_a, d_qkv, preferred_element_type=jnp.f...  107 us
  transfers between devices with their start and end apart: 90, of which 75 were waited for; matrix products, arithmetic and copies ran while one was open for 17% of the time, Pallas kernels for 0%

commit v1 on v0

v1 whole, which is shorter than its diff:
```python
import functools
import math

import jax
import jax.numpy as jnp
from jax import lax
from jax.experimental import pallas as pl
from jax.experimental.pallas import tpu as pltpu
from jax.sharding import PartitionSpec as P

NORM_EPS = 1e-6
NEG_BIG = -1e30
CHUNK = 128
F32 = jnp.float32
BF16 = jnp.bfloat16
MESH_ID = pl.DeviceIdType.MESH
GELU_A = math.sqrt(2.0 / math.pi)
GELU_B = 0.044715
VMEM_BYTES = 67043328


def dot_nn(a, b):
    return lax.dot_general(a, b, (((1,), (0,)), ((), ())), preferred_element_type=F32)


def dot_nt(a, b):
    return lax.dot_general(a, b, (((1,), (1,)), ((), ())), preferred_element_type=F32)


def dot_tn(a, b):
    return lax.dot_general(a, b, (((0,), (0,)), ((), ())), preferred_element_type=F32)


def rms_inverse(v):
    return lax.rsqrt(jnp.mean(v * v, axis=-1, keepdims=True) + NORM_EPS)


def gelu_tanh(u):
    return u * (0.5 * (1.0 + jnp.tanh(GELU_A * (u + GELU_B * (u * u * u)))))


def gelu_slope(u):
    t = jnp.tanh(GELU_A * (u + GELU_B * (u * u * u)))
    return 0.5 * (1.0 + t) + (0.5 * u) * (1.0 - t * t) * (GELU_A * (1.0 + (3.0 * GELU_B) * (u * u)))


def tile_of(width, top=512):
    for tile in (top, 384, 256, 128):
        if width % tile == 0:
            return tile
    return width


def fold_rows(v):
    total = v[0:8]
    for r in range(8, v.shape[0], 8):
        total = total + v[r : r + 8]
    return total


def step_kernel(cfg, *refs):
    n, t, tq, n_model, n_stage = cfg["n"], cfg["t"], cfg["tq"], cfg["n_model"], cfg["n_stage"]
    seq, d_model, heads, hd, ff = cfg["seq"], cfg["d_model"], cfg["heads"], cfg["hd"], cfg["ff"]
    hw = heads * hd
    elem_count = cfg["elem_count"]
    scale = hd**-0.5
    (
        x_hbm, y_hbm, wqkv_hbm, wout_hbm, wup_hbm, wdown_hbm, gain_ref,
        na_hbm, nb_hbm, at_hbm, z_hbm, dqkv_hbm, dmid_hbm, dup_hbm, dout_hbm, small_ref,
        wqkv, wout, wup, wdown, hbuf, nbbuf, doutbuf, dmidbuf, qkvbuf, upbuf, midq, yq, dkacc, dvacc,
        rs_r, rs_s, na_st, z_st, at_st, dup_st, dqkv_st, hsend, dsend, dmidq,
        lossacc, gacc, lossbuf, fin_s, fin_r,
        w_sem, x_sem, y_sem, h_rsem, h_ssem, d_rsem, d_ssem, rs_rsem, rs_ssem, ag_rsem, ag_ssem,
        out_sem, full_sem, loss_sem, fin_rsem, fin_ssem,
    ) = refs
    me = lax.axis_index("model")
    stage = lax.axis_index("stage")
    last = n_stage - 1
    order = [d for d in (2, 1, 3) if d < n_model] if n_model > 2 else list(range(1, n_model))

    def remote(src, dst, ssem, rsem, where):
        return pltpu.make_async_remote_copy(
            src_ref=src, dst_ref=dst, send_sem=ssem, recv_sem=rsem, device_id=where, device_id_type=MESH_ID
        )

    def rows_of(c):
        return pl.ds(pl.multiple_of(c * t, t), t)

    def quarter(c, m):
        return pl.ds(pl.multiple_of(c * t + m * tq, tq), tq)

    own = pl.ds(pl.multiple_of(me * tq, tq), tq)

    def weight_copy(k):
        src = (wqkv_hbm, wout_hbm, wup_hbm, wdown_hbm)[k]
        dst = (wqkv, wout, wup, wdown)[k]
        return pltpu.make_async_copy(src, dst, w_sem.at[k])

    def x_copy(c):
        return pltpu.make_async_copy(x_hbm.at[rows_of(c)], hbuf.at[rows_of(c)], x_sem.at[c])

    def y_copy(c):
        return pltpu.make_async_copy(y_hbm.at[quarter(c, me)], yq.at[c], y_sem.at[c])

    @pl.when(stage == 0)
    def _():
        x_copy(0).start()

    for k in range(4):
        weight_copy(k).start()

    @pl.when(stage == 0)
    def _():
        for c in range(1, n):
            x_copy(c).start()

    @pl.when(stage == last)
    def _():
        for c in range(n):
            y_copy(c).start()

    barrier = pltpu.get_barrier_semaphore()
    up_stage = lax.rem(stage + 1, n_stage)
    down_stage = lax.rem(stage + n_stage - 1, n_stage)
    greet = [{"model": lax.rem(me + d, n_model)} for d in range(1, n_model)]
    greet += [{"stage": up_stage, "model": m} for m in range(n_model)]
    if n_stage > 2:
        greet += [{"stage": down_stage, "model": m} for m in range(n_model)]
    for where in greet:
        pl.semaphore_signal(barrier, inc=1, device_id=where, device_id_type=MESH_ID)

    qkvbuf[...] = jnp.zeros_like(qkvbuf)
    dkacc[...] = jnp.zeros_like(dkacc)
    dvacc[...] = jnp.zeros_like(dvacc)
    lossacc[...] = jnp.zeros_like(lossacc)
    gacc[...] = jnp.zeros_like(gacc)
    pl.semaphore_wait(barrier, len(greet))

    gain_a = gain_ref[0:1, :]
    gain_b = gain_ref[1:2, :]

    def rs_copy(p, c, d, peer):
        return remote(
            rs_s.at[p, pl.ds(pl.multiple_of(peer * tq, tq), tq)], rs_r.at[p, c, d - 1],
            rs_ssem.at[p, d - 1], rs_rsem.at[p, c, d - 1], {"model": peer},
        )

    def rs_start(p, c):
        for d in order:
            rs_copy(p, c, d, lax.rem(me + d, n_model)).start()

    def rs_drain(p):
        for d in order:
            rs_copy(p, 0, d, 0).wait_send()

    def rs_sum(p, c):
        for d in order:
            rs_copy(p, c, d, 0).wait_recv()
        total = rs_s[p, own, :].astype(F32)
        for d in range(1, n_model):
            total = total + rs_r[p, c, d - 1].astype(F32)
        return total

    def ag_copy(p, buf, c, d, peer, owner):
        return remote(
            buf.at[quarter(c, owner)], buf.at[quarter(c, owner)],
            ag_ssem.at[p, d - 1], ag_rsem.at[p, c, d - 1], {"model": peer},
        )

    def ag_start(p, buf, c):
        for d in order:
            ag_copy(p, buf, c, d, lax.rem(me + d, n_model), me).start()

    def ag_drain(p, buf):
        for d in order:
            ag_copy(p, buf, 0, d, 0, 0).wait_send()

    def ag_wait(p, buf, c):
        for d in order:
            ag_copy(p, buf, c, d, 0, lax.rem(me + n_model - d, n_model)).wait_recv()

    def h_copy(c, m, sender):
        return remote(
            hsend, hbuf.at[quarter(c, sender)], h_ssem.at[m], h_rsem.at[c, sender], {"stage": up_stage, "model": m}
        )

    def d_copy(c, m, sender):
        return remote(
            dsend, doutbuf.at[quarter(c, sender)], d_ssem.at[m], d_rsem.at[c, sender],
            {"stage": down_stage, "model": m},
        )

    def peer_d_copy(c, d, peer, sender):
        return remote(
            doutbuf.at[quarter(c, sender)], doutbuf.at[quarter(c, sender)], d_ssem.at[d], d_rsem.at[c, sender],
            {"model": peer},
        )

    def staged_out(k, c):
        src = (na_st, z_st, at_st, dup_st, dqkv_st)[k]
        dst = (na_hbm, z_hbm, at_hbm, dup_hbm, dqkv_hbm)[k]
        return pltpu.make_async_copy(src, dst.at[rows_of(c)], out_sem.at[k])

    def full_out(k, c):
        src = (nbbuf, dmidbuf, doutbuf)[k]
        dst = (nb_hbm, dmid_hbm, dout_hbm)[k]
        return pltpu.make_async_copy(src.at[rows_of(c)], dst.at[rows_of(c)], full_sem.at[k, c])

    def causal(c):
        q_pos = c * t + lax.broadcasted_iota(jnp.int32, (t, seq), 0)
        k_pos = lax.broadcasted_iota(jnp.int32, (t, seq), 1)
        return k_pos <= q_pos

    def probs(c, i, mask):
        q = qkvbuf[rows_of(c), i * hd : (i + 1) * hd]
        k = qkvbuf[:, hw + i * hd : hw + (i + 1) * hd]
        s = jnp.where(mask, dot_nt(q, k) * scale, NEG_BIG)
        e = jnp.exp(s - jnp.max(s, axis=-1, keepdims=True))
        return e / jnp.sum(e, axis=-1, keepdims=True)

    def fwd_attn(c, first):
        @pl.when(stage == 0)
        def _():
            x_copy(c).wait()

        @pl.when(stage > 0)
        def _():
            for m in range(n_model):
                h_copy(c, 0, m).wait_recv()

        @pl.when(first)
        def _():
            weight_copy(0).wait()
            weight_copy(1).wait()

        @pl.when(jnp.logical_not(first))
        def _():
            staged_out(0, c).wait()
            staged_out(2, c).wait()
            rs_drain(0)

        h32 = hbuf[rows_of(c), :].astype(F32)
        na_st[...] = (h32 * rms_inverse(h32) * gain_a).astype(BF16)
        staged_out(0, c).start()
        wide = 3 * hw
        tile = tile_of(wide, 384)
        for j in range(wide // tile):
            cols = slice(j * tile, (j + 1) * tile)
            qkvbuf[rows_of(c), cols] = dot_nn(na_st[...], wqkv[:, cols]).astype(BF16)
        mask = causal(c)
        for i in range(heads):
            p16 = probs(c, i, mask).astype(BF16)
            v = qkvbuf[:, 2 * hw + i * hd : 2 * hw + (i + 1) * hd]
            at_st[:, i * hd : (i + 1) * hd] = dot_nn(p16, v).astype(BF16)
        staged_out(2, c).start()
        tile = tile_of(d_model)
        for j in range(d_model // tile):
            cols = slice(j * tile, (j + 1) * tile)
            rs_s[0, :, cols] = dot_nn(at_st[...], wout[:, cols]).astype(BF16)
        rs_start(0, c)

    def fwd_mid(c, first):
        @pl.when(jnp.logical_not(first))
        def _():
            ag_drain(0, nbbuf)

        mid = rs_sum(0, c) + hbuf[quarter(c, me), :].astype(F32)
        midq[c] = mid
        nbbuf[quarter(c, me), :] = (mid * rms_inverse(mid) * gain_b).astype(BF16)
        ag_start(0, nbbuf, c)

    def fwd_mlp(c, first):
        @pl.when(first)
        def _():
            weight_copy(2).wait()
            weight_copy(3).wait()

        @pl.when(jnp.logical_not(first))
        def _():
            staged_out(1, c).wait()
            rs_drain(1)

        ag_wait(0, nbbuf, c)
        full_out(0, c).start()
        tile = tile_of(ff)
        for j in range(ff // tile):
            cols = slice(j * tile, (j + 1) * tile)
            u = dot_nn(nbbuf[rows_of(c), :], wup[:, cols])
            upbuf[rows_of(c), cols] = u
            z_st[:, cols] = gelu_tanh(u).astype(BF16)
        staged_out(1, c).start()
        tile = tile_of(d_model)
        for j in range(d_model // tile):
            cols = slice(j * tile, (j + 1) * tile)
            rs_s[1, :, cols] = dot_nn(z_st[...], wdown[:, cols]).astype(BF16)
        rs_start(1, c)

    def fwd_end(c, first):
        h_out = (midq[c] + rs_sum(1, c)).astype(BF16)

        @pl.when(stage < last)
        def _():
            @pl.when(jnp.logical_not(first))
            def _():
                for m in range(n_model):
                    h_copy(c, m, me).wait_send()

            hsend[...] = h_out
            for m in range(n_model):
                h_copy(c, m, me).start()

        @pl.when(stage == last)
        def _():
            y_copy(c).wait()

            @pl.when(jnp.logical_not(first))
            def _():
                for d in order:
                    peer_d_copy(c, d, 0, me).wait_send()

            diff = h_out.astype(F32) - yq[c].astype(F32)
            lossacc[...] += fold_rows(diff * diff)
            doutbuf[quarter(c, me), :] = (diff * (1.0 / elem_count)).astype(BF16)
            for d in order:
                peer_d_copy(c, d, lax.rem(me + d, n_model), me).start()

    def fwd_body(i, carry):
        first = i == 0
        second = i == 1

        @pl.when(i < n)
        def _():
            fwd_attn(i, first)

        @pl.when(i >= 1)
        def _():
            fwd_mlp(i - 1, second)

        @pl.when(i < n)
        def _():
            fwd_mid(i, first)

        @pl.when(i >= 1)
        def _():
            fwd_end(i - 1, second)

        return carry

    lax.fori_loop(0, n + 1, fwd_body, 0)

    rs_drain(0)
    rs_drain(1)
    ag_drain(0, nbbuf)
    staged_out(0, 0).wait()
    staged_out(1, 0).wait()
    staged_out(2, 0).wait()

    @pl.when(stage < last)
    def _():
        for m in range(n_model):
            h_copy(0, m, me).wait_send()

    @pl.when(stage == last)
    def _():
        for d in order:
            peer_d_copy(0, d, 0, me).wait_send()
        total = lossacc[:, 0:128]
        for j in range(1, d_model // 128):
            total = total + lossacc[:, j * 128 : (j + 1) * 128]
        lossbuf[...] = total

    def rms_backward(v, gain, d_norm, k):
        inv = rms_inverse(v)
        normed = v * inv
        gacc[k] += fold_rows(d_norm * normed)
        d_normed = d_norm * gain
        return inv * (d_normed - normed * jnp.mean(d_normed * normed, axis=-1, keepdims=True))

    def bwd_mlp(c, first):
        @pl.when(stage < last)
        def _():
            for m in range(n_model):
                d_copy(c, 0, m).wait_recv()

        @pl.when(stage == last)
        def _():
            for d in order:
                peer_d_copy(c, d, 0, lax.rem(me + n_model - d, n_model)).wait_recv()

        full_out(2, c).start()

        @pl.when(jnp.logical_not(first))
        def _():
            staged_out(3, c).wait()
            rs_drain(2)

        tile = tile_of(ff)
        for j in range(ff // tile):
            cols = slice(j * tile, (j + 1) * tile)
            d_gelu = dot_nt(doutbuf[rows_of(c), :], wdown[cols, :])
            dup_st[:, cols] = (d_gelu * gelu_slope(upbuf[rows_of(c), cols])).astype(BF16)
        staged_out(3, c).start()
        tile = tile_of(d_model)
        for j in range(d_model // tile):
            cols = slice(j * tile, (j + 1) * tile)
            rs_s[2, :, cols] = dot_nt(dup_st[...], wup[cols, :]).astype(BF16)
        rs_start(2, c)

    def bwd_mid(c, first, slot):
        @pl.when(jnp.logical_not(first))
        def _():
            ag_drain(1, dmidbuf)

        d_norm = rs_sum(2, c)
        d_mid = doutbuf[quarter(c, me), :].astype(F32) + rms_backward(midq[c], gain_b, d_norm, 1)
        dmidq[slot] = d_mid
        dmidbuf[quarter(c, me), :] = d_mid.astype(BF16)
        ag_start(1, dmidbuf, c)

    def bwd_attn(c, first):
        ag_wait(1, dmidbuf, c)
        full_out(1, c).start()

        @pl.when(jnp.logical_not(first))
        def _():
            staged_out(4, c).wait()
            rs_drain(3)

        d_attn = dot_nt(dmidbuf[rows_of(c), :], wout[...]).astype(BF16)
        mask = causal(c)
        for i in range(heads):
            qc = slice(i * hd, (i + 1) * hd)
            kc = slice(hw + i * hd, hw + (i + 1) * hd)
            vc = slice(2 * hw + i * hd, 2 * hw + (i + 1) * hd)
            da = d_attn[:, qc]
            p = probs(c, i, mask)
            dp = dot_nt(da, qkvbuf[:, vc])
            ds = (p * (dp - jnp.sum(p * dp, axis=-1, keepdims=True)) * scale).astype(BF16)
            dqkv_st[:, qc] = dot_nn(ds, qkvbuf[:, kc]).astype(BF16)
            dkacc[:, qc] += dot_tn(ds, qkvbuf[rows_of(c), qc])
            dvacc[:, qc] += dot_tn(p.astype(BF16), da)
        dqkv_st[:, hw : 2 * hw] = dkacc[rows_of(c), :].astype(BF16)
        dqkv_st[:, 2 * hw : 3 * hw] = dvacc[rows_of(c), :].astype(BF16)
        staged_out(4, c).start()
        tile = tile_of(d_model)
        for j in range(d_model // tile):
            cols = slice(j * tile, (j + 1) * tile)
            rs_s[3, :, cols] = dot_nt(dqkv_st[...], wqkv[cols, :]).astype(BF16)
        rs_start(3, c)

    def loss_copy():
        return remote(lossbuf, lossbuf, loss_sem.at[0], loss_sem.at[1], {"stage": down_stage})

    def bwd_end(c, first, slot):
        h32 = hbuf[quarter(c, me), :].astype(F32)
        d_in = dmidq[slot] + rms_backward(h32, gain_a, rs_sum(3, c), 0)

        @pl.when(stage > 0)
        def _():
            @pl.when(jnp.logical_not(first))
            def _():
                for m in range(n_model):
                    d_copy(c, m, me).wait_send()

            dsend[...] = d_in.astype(BF16)
            for m in range(n_model):
                d_copy(c, m, me).start()

        @pl.when(first)
        def _():
            @pl.when(stage < last)
            def _():
                loss_copy().wait_recv()

            @pl.when(stage > 0)
            def _():
                loss_copy().start()

    def bwd_body(i, carry):
        first = i == 0
        second = i == 1
        c = n - 1 - i

        @pl.when(i < n)
        def _():
            bwd_mlp(c, first)

        @pl.when(i >= 1)
        def _():
            bwd_attn(c + 1, second)

        @pl.when(i < n)
        def _():
            bwd_mid(c, first, lax.rem(i, 2))

        @pl.when(i >= 1)
        def _():
            bwd_end(c + 1, second, lax.rem(i + 1, 2))

        return carry

    lax.fori_loop(0, n + 1, bwd_body, 0)

    fin_s[...] = jnp.zeros_like(fin_s)
    fin_s[0:1, :] = jnp.sum(gacc[0], axis=0, keepdims=True)
    fin_s[1:2, :] = jnp.sum(gacc[1], axis=0, keepdims=True)
    fin_s[2:3, 0:128] = jnp.sum(lossbuf[...], axis=0, keepdims=True)

    def fin_copy(d, peer):
        return remote(fin_s, fin_r.at[d - 1], fin_ssem.at[d - 1], fin_rsem.at[d - 1], {"model": peer})

    for d in order:
        fin_copy(d, lax.rem(me + d, n_model)).start()

    rs_drain(2)
    rs_drain(3)
    ag_drain(1, dmidbuf)
    staged_out(3, 0).wait()
    staged_out(4, 0).wait()
    for k in range(3):
        for c in range(n):
            full_out(k, c).wait()

    @pl.when(stage > 0)
    def _():
        for m in range(n_model):
            d_copy(0, m, me).wait_send()
        loss_copy().wait_send()

    for d in order:
        fin_copy(d, 0).wait_recv()
    parts = [jnp.where(me == 0, fin_s[...], 0.0)]
    for m in range(n_model):
        term = jnp.where(me == m, fin_s[...], 0.0)
        for d in range(1, n_model):
            term = term + jnp.where(lax.rem(m + d, n_model) == me, fin_r[d - 1], 0.0)
        parts.append(term)
    total = parts[1]
    for m in range(1, n_model):
        total = total + parts[m + 1]
    small_ref[0:2, :] = total[0:2, :]
    loss = jnp.sum(total[2:3, :], axis=-1, keepdims=True) * (0.5 / elem_count)
    small_ref[2:8, :] = jnp.broadcast_to(loss, (6, d_model))
    for d in order:
        fin_copy(d, 0).wait_send()


def run_step(cfg, x, y, wqkv, wout, wup, wdown, gain):
    n, t, tq, n_model, seq = cfg["n"], cfg["t"], cfg["tq"], cfg["n_model"], cfg["seq"]
    d_model, ff, hw = cfg["d_model"], cfg["ff"], cfg["heads"] * cfg["hd"]
    dma = pltpu.SemaphoreType.DMA
    near = max(n_model - 1, 1)
    act = lambda width: jax.ShapeDtypeStruct((seq, width), BF16)
    any_spec = pl.BlockSpec(memory_space=pl.ANY)
    vmem_spec = pl.BlockSpec(memory_space=pltpu.VMEM)
    scratch = [
        pltpu.VMEM((d_model, 3 * hw), BF16),
        pltpu.VMEM((hw, d_model), BF16),
        pltpu.VMEM((d_model, ff), BF16),
        pltpu.VMEM((ff, d_model), BF16),
        pltpu.VMEM((seq, d_model), BF16),
        pltpu.VMEM((seq, d_model), BF16),
        pltpu.VMEM((seq, d_model), BF16),
        pltpu.VMEM((seq, d_model), BF16),
        pltpu.VMEM((seq, 3 * hw), BF16),
        pltpu.VMEM((seq, ff), F32),
        pltpu.VMEM((n, tq, d_model), F32),
        pltpu.VMEM((n, tq, d_model), BF16),
        pltpu.VMEM((seq, hw), F32),
        pltpu.VMEM((seq, hw), F32),
        pltpu.VMEM((4, n, near, tq, d_model), BF16),
        pltpu.VMEM((4, t, d_model), BF16),
        pltpu.VMEM((t, d_model), BF16),
        pltpu.VMEM((t, ff), BF16),
        pltpu.VMEM((t, hw), BF16),
        pltpu.VMEM((t, ff), BF16),
        pltpu.VMEM((t, 3 * hw), BF16),
        pltpu.VMEM((tq, d_model), BF16),
        pltpu.VMEM((tq, d_model), BF16),
        pltpu.VMEM((2, tq, d_model), F32),
        pltpu.VMEM((8, d_model), F32),
        pltpu.VMEM((2, 8, d_model), F32),
        pltpu.VMEM((8, 128), F32),
        pltpu.VMEM((8, d_model), F32),
        pltpu.VMEM((near, 8, d_model), F32),
        dma((4,)),
        dma((n,)),
        dma((n,)),
        dma((n, n_model)),
        dma((n_model,)),
        dma((n, n_model)),
        dma((n_model,)),
        dma((4, n, near)),
        dma((4, near)),
        dma((2, n, near)),
        dma((2, near)),
        dma((5,)),
        dma((3, n)),
        dma((2,)),
        dma((near,)),
        dma((near,)),
    ]
    return pl.pallas_call(
        functools.partial(step_kernel, cfg),
        name="pipeline_step",
        out_shape=(
            act(d_model), act(d_model), act(hw), act(ff), act(3 * hw), act(d_model), act(ff), act(d_model),
            jax.ShapeDtypeStruct((8, d_model), F32),
        ),
        in_specs=[any_spec] * 6 + [vmem_spec],
        out_specs=[any_spec] * 8 + [vmem_spec],
        scratch_shapes=scratch,
        compiler_params=pltpu.CompilerParams(
            collective_id=0, has_side_effects=True, vmem_limit_bytes=VMEM_BYTES
        ),
    )(x, y, wqkv, wout, wup, wdown, gain)


def solution(mesh):
    n_stage = mesh.shape["stage"]
    n_model = mesh.shape["model"]

    def device_fn(x_in, y_target, w_qkv, w_out, w_up, w_down, norm_gain):
        n_batch, seq_len, d_model = x_in.shape
        heads, hd, ff = w_qkv.shape[3], w_qkv.shape[4], w_up.shape[2]
        t = min(CHUNK, seq_len)
        cfg = dict(
            n=seq_len // t, t=t, tq=t // n_model, n_model=n_model, n_stage=n_stage, seq=seq_len, d_model=d_model,
            heads=heads, hd=hd, ff=ff, elem_count=n_batch * seq_len * d_model,
        )
        na, nb, at, z, dqkv, dmid, dup, dout, small = run_step(
            cfg, x_in[0], y_target[0], w_qkv[0].reshape(d_model, 3 * heads * hd), w_out[0].reshape(heads * hd, d_model),
            w_up[0], w_down[0], norm_gain[0].astype(F32),
        )
        grad_qkv = dot_tn(na, dqkv).reshape(1, d_model, 3, heads, hd)
        grad_out = dot_tn(at, dmid).reshape(1, heads, hd, d_model)
        grad_up = dot_tn(nb, dup)[None]
        grad_down = dot_tn(z, dout)[None]
        return small[2:3, 0], grad_qkv, grad_out, grad_up, grad_down, small[None, 0:2]

    act_spec = P("data", None, None)
    weight_specs = (
        P("stage", None, None, "model", None),
        P("stage", "model", None, None),
        P("stage", None, "model"),
        P("stage", "model", None),
        P("stage", None, None),
    )
    grad_specs = (
        P(("data", "stage"), None, None, "model", None),
        P(("data", "stage"), "model", None, None),
        P(("data", "stage"), None, "model"),
        P(("data", "stage"), "model", None),
        P(("data", "stage"), None, None),
    )
    return jax.shard_map(
        device_fn,
        mesh=mesh,
        in_specs=(act_spec, act_spec) + weight_specs,
        out_specs=(P("data"),) + grad_specs,
        check_vma=False,
    )
```

time: 3750 us -> 866 us (0.23)
  waiting for transfers between devices: 1970 us -> 0 us
  matrix products: 1160 us -> 28.9 us
  Pallas kernels: 0 us -> 816 us
  other arithmetic: 334 us -> 1.3 us
  local copies, waits for them, and re-layouts: 154 us -> 18.7 us
  starting transfers between devices: 41.4 us -> 0 us
    psum x60 -> x0, waiting for transfers between devices: 1930 us -> none  [the longest x15 619 us: layer_forward(): mid_hid = h32 + lax.psum(attn_part, 'model')]
    dot_general x255 -> x4, matrix products: 1070 us -> 28.9 us  [dot_tn(): lax.dot_general(a, b, (((0,), (0,)), ((), ())), preferred_element_type=F32)]
    pallas_call x0 -> x1, Pallas kernels: none -> 816 us  [run_step(): pl.pallas_call(functools.partial(step_kernel, cfg), name='pipeline_step',...]
    reduce_sum x105 -> x0, other arithmetic: 140 us -> none  [the longest x60 61 us: rms_inverse(): return lax.rsqrt(jnp.mean(hid32 * hid32, axis=-1, keepdims=True) + NORM_EPS)]
    dynamic_update_slice x75 -> x0, other arithmetic: 122 us -> none  [the longest x60 96.6 us: store_at(): lax.dynamic_update_index_in_dim(buf_all, jnp.where(is_valid, new_val, old...]
    dynamic_slice x105 -> x0, local copies, waits for them, and re-layouts: 117 us -> none  [the longest x75 81 us: store_at(): old_val = lax.dynamic_index_in_dim(buf_all, index, 0, keepdims=False)]
    sub x30 -> x0, matrix products: 89.8 us -> none  [causal_probs(): return jax.nn.softmax(scores, axis=-1)]
    ppermute x30 -> x0, starting transfers between devices: 39.4 us -> none  [the longest x15 19.8 us: fwd_tick(): recv_act = lax.ppermute(h_out, 'stage', fwd_perm)]
  transfers between devices with their start and end apart: 90 -> 0, of which waited for: 75 -> 0; matrix products, arithmetic and copies ran while one was open for 17% -> 0% of each run, Pallas kernels for 0% -> 0%
where the time goes in v1:
time: 866 us
  Pallas kernels  816 us (94%)
  matrix products  28.9 us (3%)
  local copies, waits for them, and re-layouts  18.7 us (2%)
    pallas_call x1, Pallas kernels, run_step(): pl.pallas_call(functools.partial(step_kernel, cfg), name='pipeline_step',...  816 us
    dot_general x4, matrix products, dot_tn(): lax.dot_general(a, b, (((0,), (0,)), ((), ())), preferred_element_type=F32)  28.9 us

profile of v1, /device:TPU:96, one launch (start us, length us, event | category | flops | bytes accessed | tf_op | source)
XLA Modules:
  0.0 865.7 jit_solution(4902184422898018063)
XLA Ops:
  0.6 1.3 bitcast_convert_fusion.refs_6_
  1.9 4.3 copy.15
  6.2 3.7 copy.16.refs_2_
  9.9 816.1 %pipeline_step.1 = (bf16[1024,1536]{1,0:T(8,128)(2,1)}, bf16[1024,1536]{1,0:T(8,128)(2,1)}, bf16[1024,384]{1,0:T(8,128)(2,1)}, bf16[1024,1536]{1,0:T(8,128)(2,1)...) custom-call(bf16[1024,1536]{1,0:T(8,128)(2,1)} %bitcast.30, ...), custom_call_target="tpu_custom_call" | custom-call | tf_op jit(solution)/shard_map/pipeline_step/pallas_call | solution.py:603
  826.0 1.2 slice.6
  827.1 1.4 slice_bitcast_fusion
  828.5 9.5 %fusion = f32[1536,1152]{0,1:T(8,128)} fusion(bf16[1024,1536]{1,0:T(8,128)(2,1)} %get-tuple-element.16, bf16[1024,1152]{1,0:T(8,128)(2,1)} %get-tuple-element.17), kind=kOutput, calls=%fused_computation.4 | convolution fusion | flops 3623878656 | bytes 12582912 | tf_op jit(solution)/shard_map/dot_general | solution.py:31
  838.0 0.0 copy-start.4
  838.0 8.2 copy.17
  846.2 0.0 copy-done.4
  846.2 0.0 copy-start.2
  846.2 0.0 copy-start.3
  846.2 4.1 fusion.1
  850.3 0.0 copy-done.2
  850.3 0.0 copy-done.3
  850.3 0.0 copy-start
  850.3 0.0 copy-start.1
  850.3 7.8 convolution_bitcast_fusion.1
  858.1 0.0 copy-done
  858.1 0.0 copy-done.1
  858.1 7.6 convolution_bitcast_fusion
Async XLA Ops:
  838.0 8.2 copy-start.4
  846.2 4.1 copy-start.2
  846.2 4.1 copy-start.3
  850.3 7.8 copy-start
  850.3 7.8 copy-start.1

commit v2 on v1

--- a/solution.py
+++ b/solution.py
@@ -10,7 +10,10 @@
 
 NORM_EPS = 1e-6
 NEG_BIG = -1e30
-CHUNK = 128
+CHUNK = 64
+KEY_STEP = 256
+GRAD_ROWS = 768
+LOG2E = 1.4426950408889634
 F32 = jnp.float32
 BF16 = jnp.bfloat16
 MESH_ID = pl.DeviceIdType.MESH
@@ -45,7 +48,7 @@
 
 
 def tile_of(width, top=512):
-    for tile in (top, 384, 256, 128):
+    for tile in (top, 512, 384, 256, 128):
         if width % tile == 0:
             return tile
     return width
@@ -67,7 +70,7 @@
     (
         x_hbm, y_hbm, wqkv_hbm, wout_hbm, wup_hbm, wdown_hbm, gain_ref,
         na_hbm, nb_hbm, at_hbm, z_hbm, dqkv_hbm, dmid_hbm, dup_hbm, dout_hbm, small_ref,
-        wqkv, wout, wup, wdown, hbuf, nbbuf, doutbuf, dmidbuf, qkvbuf, upbuf, midq, yq, dkacc, dvacc,
+        wqkv, wout, wup, wdown, wqkv_t, wout_t, wup_t, wdown_t, hbuf, nbbuf, doutbuf, dmidbuf, qkvbuf, upbuf, midq, yq, dkacc, dvacc,
         rs_r, rs_s, na_st, z_st, at_st, dup_st, dqkv_st, hsend, dsend, dmidq,
         lossacc, gacc, lossbuf, fin_s, fin_r,
         w_sem, x_sem, y_sem, h_rsem, h_ssem, d_rsem, d_ssem, rs_rsem, rs_ssem, ag_rsem, ag_ssem,
@@ -91,9 +94,13 @@
 
     own = pl.ds(pl.multiple_of(me * tq, tq), tq)
 
+    slabs = 3 * heads
+
     def weight_copy(k):
-        src = (wqkv_hbm, wout_hbm, wup_hbm, wdown_hbm)[k]
-        dst = (wqkv, wout, wup, wdown)[k]
+        if k < slabs:
+            return pltpu.make_async_copy(wqkv_hbm.at[k], wqkv.at[:, pl.ds(k * hd, hd)], w_sem.at[k])
+        src = (wout_hbm, wup_hbm, wdown_hbm)[k - slabs]
+        dst = (wout, wup, wdown)[k - slabs]
         return pltpu.make_async_copy(src, dst, w_sem.at[k])
 
     def x_copy(c):
@@ -106,7 +113,7 @@
     def _():
         x_copy(0).start()
 
-    for k in range(4):
+    for k in range(slabs + 3):
         weight_copy(k).start()
 
     @pl.when(stage == 0)
@@ -129,36 +136,37 @@
     for where in greet:
         pl.semaphore_signal(barrier, inc=1, device_id=where, device_id_type=MESH_ID)
 
-    qkvbuf[...] = jnp.zeros_like(qkvbuf)
-    dkacc[...] = jnp.zeros_like(dkacc)
-    dvacc[...] = jnp.zeros_like(dvacc)
+    qkvbuf[:, 2 * hw : 3 * hw] = jnp.zeros((seq, hw), BF16)
     lossacc[...] = jnp.zeros_like(lossacc)
     gacc[...] = jnp.zeros_like(gacc)
     pl.semaphore_wait(barrier, len(greet))
 
-    gain_a = gain_ref[0:1, :]
-    gain_b = gain_ref[1:2, :]
+    gains = gain_ref[...].astype(F32)
+    gain_a = gains[0:1, :]
+    gain_b = gains[1:2, :]
 
     def rs_copy(p, c, d, peer):
+        slot = lax.rem(c, 2)
         return remote(
-            rs_s.at[p, pl.ds(pl.multiple_of(peer * tq, tq), tq)], rs_r.at[p, c, d - 1],
-            rs_ssem.at[p, d - 1], rs_rsem.at[p, c, d - 1], {"model": peer},
+            rs_s.at[p, slot, pl.ds(pl.multiple_of(peer * tq, tq), tq)], rs_r.at[p % 2, c, d - 1],
+            rs_ssem.at[p, slot, d - 1], rs_rsem.at[p, c, d - 1], {"model": peer},
         )
 
     def rs_start(p, c):
         for d in order:
             rs_copy(p, c, d, lax.rem(me + d, n_model)).start()
 
-    def rs_drain(p):
+    def rs_drain(p, c):
         for d in order:
-            rs_copy(p, 0, d, 0).wait_send()
+            rs_copy(p, c, d, 0).wait_send()
 
     def rs_sum(p, c):
-        for d in order:
-            rs_copy(p, c, d, 0).wait_recv()
-        total = rs_s[p, own, :].astype(F32)
+        with jax.named_scope(f"rs_wait{p}"):
+            for d in order:
+                rs_copy(p, c, d, 0).wait_recv()
+        total = rs_s[p, lax.rem(c, 2), own, :].astype(F32)
         for d in range(1, n_model):
-            total = total + rs_r[p, c, d - 1].astype(F32)
+            total = total + rs_r[p % 2, c, d - 1].astype(F32)
         return total
 
     def ag_copy(p, buf, c, d, peer, owner):
@@ -176,8 +184,9 @@
             ag_copy(p, buf, 0, d, 0, 0).wait_send()
 
     def ag_wait(p, buf, c):
-        for d in order:
-            ag_copy(p, buf, c, d, 0, lax.rem(me + n_model - d, n_model)).wait_recv()
+        with jax.named_scope(f"ag_wait{p}"):
+            for d in order:
+                ag_copy(p, buf, c, d, 0, lax.rem(me + n_model - d, n_model)).wait_recv()
 
     def h_copy(c, m, sender):
         return remote(
@@ -206,17 +215,28 @@
         dst = (nb_hbm, dmid_hbm, dout_hbm)[k]
         return pltpu.make_async_copy(src.at[rows_of(c)], dst.at[rows_of(c)], full_sem.at[k, c])
 
-    def causal(c):
-        q_pos = c * t + lax.broadcasted_iota(jnp.int32, (t, seq), 0)
-        k_pos = lax.broadcasted_iota(jnp.int32, (t, seq), 1)
-        return k_pos <= q_pos
-
-    def probs(c, i, mask):
-        q = qkvbuf[rows_of(c), i * hd : (i + 1) * hd]
-        k = qkvbuf[:, hw + i * hd : hw + (i + 1) * hd]
-        s = jnp.where(mask, dot_nt(q, k) * scale, NEG_BIG)
-        e = jnp.exp(s - jnp.max(s, axis=-1, keepdims=True))
-        return e / jnp.sum(e, axis=-1, keepdims=True)
+    key_step = min(KEY_STEP, seq)
+
+    def by_prefix(c, body):
+        need = lax.div(c * t + t - 1, key_step)
+        for k in range(seq // key_step):
+
+            @pl.when(need == k)
+            def _():
+                body((k + 1) * key_step)
+
+    def scores(c, keys):
+        return [
+            dot_nt(qkvbuf[rows_of(c), i * hd : (i + 1) * hd], qkvbuf[0:keys, hw + i * hd : hw + (i + 1) * hd])
+            for i in range(heads)
+        ]
+
+    def causal_softmax(c, keys, raw):
+        q_pos = c * t + lax.broadcasted_iota(jnp.int32, (t, keys), 0)
+        k_pos = lax.broadcasted_iota(jnp.int32, (t, keys), 1)
+        s = jnp.where(k_pos <= q_pos, raw, NEG_BIG / scale)
+        e = jnp.exp2((s - jnp.max(s, axis=-1, keepdims=True)) * (scale * LOG2E))
+        return e * (1.0 / jnp.sum(e, axis=-1, keepdims=True))
 
     def fwd_attn(c, first):
         @pl.when(stage == 0)
@@ -225,19 +245,25 @@
 
         @pl.when(stage > 0)
         def _():
-            for m in range(n_model):
-                h_copy(c, 0, m).wait_recv()
-
-        @pl.when(first)
-        def _():
-            weight_copy(0).wait()
-            weight_copy(1).wait()
+            with jax.named_scope("h_wait"):
+                for m in range(n_model):
+                    h_copy(c, 0, m).wait_recv()
+
+        @pl.when(first & (stage == 0))
+        def _():
+            for k in range(slabs + 1):
+                weight_copy(k).wait()
 
         @pl.when(jnp.logical_not(first))
         def _():
             staged_out(0, c).wait()
             staged_out(2, c).wait()
-            rs_drain(0)
+
+        @pl.when(c >= 2)
+        def _():
+            rs_drain(0, c)
+
+        slot = lax.rem(c, 2)
 
         h32 = hbuf[rows_of(c), :].astype(F32)
         na_st[...] = (h32 * rms_inverse(h32) * gain_a).astype(BF16)
@@ -247,16 +273,19 @@
         for j in range(wide // tile):
             cols = slice(j * tile, (j + 1) * tile)
             qkvbuf[rows_of(c), cols] = dot_nn(na_st[...], wqkv[:, cols]).astype(BF16)
-        mask = causal(c)
-        for i in range(heads):
-            p16 = probs(c, i, mask).astype(BF16)
-            v = qkvbuf[:, 2 * hw + i * hd : 2 * hw + (i + 1) * hd]
-            at_st[:, i * hd : (i + 1) * hd] = dot_nn(p16, v).astype(BF16)
+
+        def attend(keys):
+            probs = [causal_softmax(c, keys, raw).astype(BF16) for raw in scores(c, keys)]
+            for i in range(heads):
+                v = qkvbuf[0:keys, 2 * hw + i * hd : 2 * hw + (i + 1) * hd]
+                at_st[:, i * hd : (i + 1) * hd] = dot_nn(probs[i], v).astype(BF16)
+
+        by_prefix(c, attend)
         staged_out(2, c).start()
         tile = tile_of(d_model)
         for j in range(d_model // tile):
             cols = slice(j * tile, (j + 1) * tile)
-            rs_s[0, :, cols] = dot_nn(at_st[...], wout[:, cols]).astype(BF16)
+            rs_s[0, slot, :, cols] = dot_nn(at_st[...], wout[:, cols]).astype(BF16)
         rs_start(0, c)
 
     def fwd_mid(c, first):
@@ -270,15 +299,20 @@
         ag_start(0, nbbuf, c)
 
     def fwd_mlp(c, first):
-        @pl.when(first)
-        def _():
-            weight_copy(2).wait()
-            weight_copy(3).wait()
+        @pl.when(first & (stage == 0))
+        def _():
+            weight_copy(slabs + 1).wait()
+            weight_copy(slabs + 2).wait()
 
         @pl.when(jnp.logical_not(first))
         def _():
             staged_out(1, c).wait()
-            rs_drain(1)
+
+        @pl.when(c >= 2)
+        def _():
+            rs_drain(1, c)
+
+        slot = lax.rem(c, 2)
 
         ag_wait(0, nbbuf, c)
         full_out(0, c).start()
@@ -292,7 +326,7 @@
         tile = tile_of(d_model)
         for j in range(d_model // tile):
             cols = slice(j * tile, (j + 1) * tile)
-            rs_s[1, :, cols] = dot_nn(z_st[...], wdown[:, cols]).astype(BF16)
+            rs_s[1, slot, :, cols] = dot_nn(z_st[...], wdown[:, cols]).astype(BF16)
         rs_start(1, c)
 
     def fwd_end(c, first):
@@ -324,32 +358,49 @@
             for d in order:
                 peer_d_copy(c, d, lax.rem(me + d, n_model), me).start()
 
-    def fwd_body(i, carry):
-        first = i == 0
-        second = i == 1
-
-        @pl.when(i < n)
-        def _():
-            fwd_attn(i, first)
-
-        @pl.when(i >= 1)
-        def _():
-            fwd_mlp(i - 1, second)
-
-        @pl.when(i < n)
-        def _():
-            fwd_mid(i, first)
-
-        @pl.when(i >= 1)
-        def _():
-            fwd_end(i - 1, second)
-
-        return carry
-
-    lax.fori_loop(0, n + 1, fwd_body, 0)
-
-    rs_drain(0)
-    rs_drain(1)
+    def pipeline(phases, chunk_of):
+        deepest = max(lag for _, lag, _ in phases)
+
+        def body(i, carry):
+            for phase, lag, name in phases:
+                j = i - lag
+
+                @pl.when((j >= 0) & (j < n))
+                def _():
+                    with jax.named_scope(name):
+                        phase(chunk_of(j), j == 0)
+
+            return carry
+
+        lax.fori_loop(0, n + deepest, body, 0)
+
+    def flip_weights():
+        for w, w_t in ((wdown, wdown_t), (wup, wup_t), (wout, wout_t), (wqkv, wqkv_t)):
+            depth = tile_of(w.shape[0], 256)
+            for r in range(w.shape[0] // depth):
+                w_t[:, r * depth : (r + 1) * depth] = w[r * depth : (r + 1) * depth, :].T
+
+    @pl.when(stage > 0)
+    def _():
+        for k in range(slabs + 3):
+            weight_copy(k).wait()
+        flip_weights()
+
+    pipeline(
+        [(fwd_attn, 0, "fwd_attn"), (fwd_mlp, 1, "fwd_mlp"), (fwd_mid, 0, "fwd_mid"), (fwd_end, 1, "fwd_end")],
+        lambda j: j,
+    )
+
+    @pl.when(stage == 0)
+    def _():
+        flip_weights()
+
+    dkacc[...] = jnp.zeros_like(dkacc)
+    dvacc[...] = jnp.zeros_like(dvacc)
+
+    for c in range(min(n, 2)):
+        rs_drain(0, c)
+        rs_drain(1, c)
     ag_drain(0, nbbuf)
     staged_out(0, 0).wait()
     staged_out(1, 0).wait()
@@ -379,8 +430,9 @@
     def bwd_mlp(c, first):
         @pl.when(stage < last)
         def _():
-            for m in range(n_model):
-                d_copy(c, 0, m).wait_recv()
+            with jax.named_scope("d_wait"):
+                for m in range(n_model):
+                    d_copy(c, 0, m).wait_recv()
 
         @pl.when(stage == last)
         def _():
@@ -392,28 +444,33 @@
         @pl.when(jnp.logical_not(first))
         def _():
             staged_out(3, c).wait()
-            rs_drain(2)
+
+        @pl.when(c < n - 2)
+        def _():
+            rs_drain(2, c)
+
+        slot = lax.rem(c, 2)
 
         tile = tile_of(ff)
         for j in range(ff // tile):
             cols = slice(j * tile, (j + 1) * tile)
-            d_gelu = dot_nt(doutbuf[rows_of(c), :], wdown[cols, :])
+            d_gelu = dot_nn(doutbuf[rows_of(c), :], wdown_t[:, cols])
             dup_st[:, cols] = (d_gelu * gelu_slope(upbuf[rows_of(c), cols])).astype(BF16)
         staged_out(3, c).start()
         tile = tile_of(d_model)
         for j in range(d_model // tile):
             cols = slice(j * tile, (j + 1) * tile)
-            rs_s[2, :, cols] = dot_nt(dup_st[...], wup[cols, :]).astype(BF16)
+            rs_s[2, slot, :, cols] = dot_nn(dup_st[...], wup_t[:, cols]).astype(BF16)
         rs_start(2, c)
 
-    def bwd_mid(c, first, slot):
+    def bwd_mid(c, first):
         @pl.when(jnp.logical_not(first))
         def _():
             ag_drain(1, dmidbuf)
 
         d_norm = rs_sum(2, c)
         d_mid = doutbuf[quarter(c, me), :].astype(F32) + rms_backward(midq[c], gain_b, d_norm, 1)
-        dmidq[slot] = d_mid
+        dmidq[lax.rem(c, 4)] = d_mid
         dmidbuf[quarter(c, me), :] = d_mid.astype(BF16)
         ag_start(1, dmidbuf, c)
 
@@ -424,36 +481,51 @@
         @pl.when(jnp.logical_not(first))
         def _():
             staged_out(4, c).wait()
-            rs_drain(3)
-
-        d_attn = dot_nt(dmidbuf[rows_of(c), :], wout[...]).astype(BF16)
-        mask = causal(c)
-        for i in range(heads):
-            qc = slice(i * hd, (i + 1) * hd)
-            kc = slice(hw + i * hd, hw + (i + 1) * hd)
-            vc = slice(2 * hw + i * hd, 2 * hw + (i + 1) * hd)
-            da = d_attn[:, qc]
-            p = probs(c, i, mask)
-            dp = dot_nt(da, qkvbuf[:, vc])
-            ds = (p * (dp - jnp.sum(p * dp, axis=-1, keepdims=True)) * scale).astype(BF16)
-            dqkv_st[:, qc] = dot_nn(ds, qkvbuf[:, kc]).astype(BF16)
-            dkacc[:, qc] += dot_tn(ds, qkvbuf[rows_of(c), qc])
-            dvacc[:, qc] += dot_tn(p.astype(BF16), da)
+
+        @pl.when(c < n - 2)
+        def _():
+            rs_drain(3, c)
+
+        slot = lax.rem(c, 2)
+
+        d_attn = dot_nn(dmidbuf[rows_of(c), :], wout_t[...]).astype(BF16)
+        at_st[...] = d_attn
+
+        def attend(keys):
+            raws = scores(c, keys)
+            d_probs = [
+                dot_nt(at_st[:, i * hd : (i + 1) * hd], qkvbuf[0:keys, 2 * hw + i * hd : 2 * hw + (i + 1) * hd])
+                for i in range(heads)
+            ]
+            probs, d_scores = [], []
+            for raw, dp in zip(raws, d_probs):
+                p = causal_softmax(c, keys, raw)
+                probs.append(p.astype(BF16))
+                d_scores.append((p * (dp - jnp.sum(p * dp, axis=-1, keepdims=True)) * scale).astype(BF16))
+            for i in range(heads):
+                cols = slice(i * hd, (i + 1) * hd)
+                dqkv_st[:, cols] = dot_nn(d_scores[i], qkvbuf[0:keys, hw + i * hd : hw + (i + 1) * hd]).astype(BF16)
+            for i in range(heads):
+                cols = slice(i * hd, (i + 1) * hd)
+                dkacc[0:keys, cols] += dot_tn(d_scores[i], qkvbuf[rows_of(c), cols])
+                dvacc[0:keys, cols] += dot_tn(probs[i], at_st[:, cols])
+
+        by_prefix(c, attend)
         dqkv_st[:, hw : 2 * hw] = dkacc[rows_of(c), :].astype(BF16)
         dqkv_st[:, 2 * hw : 3 * hw] = dvacc[rows_of(c), :].astype(BF16)
         staged_out(4, c).start()
         tile = tile_of(d_model)
         for j in range(d_model // tile):
             cols = slice(j * tile, (j + 1) * tile)
-            rs_s[3, :, cols] = dot_nt(dqkv_st[...], wqkv[cols, :]).astype(BF16)
+            rs_s[3, slot, :, cols] = dot_nn(dqkv_st[...], wqkv_t[:, cols]).astype(BF16)
         rs_start(3, c)
 
     def loss_copy():
         return remote(lossbuf, lossbuf, loss_sem.at[0], loss_sem.at[1], {"stage": down_stage})
 
-    def bwd_end(c, first, slot):
+    def bwd_end(c, first):
         h32 = hbuf[quarter(c, me), :].astype(F32)
-        d_in = dmidq[slot] + rms_backward(h32, gain_a, rs_sum(3, c), 0)
+        d_in = dmidq[lax.rem(c, 4)] + rms_backward(h32, gain_a, rs_sum(3, c), 0)
 
         @pl.when(stage > 0)
         def _():
@@ -476,30 +548,10 @@
             def _():
                 loss_copy().start()
 
-    def bwd_body(i, carry):
-        first = i == 0
-        second = i == 1
-        c = n - 1 - i
-
-        @pl.when(i < n)
-        def _():
-            bwd_mlp(c, first)
-
-        @pl.when(i >= 1)
-        def _():
-            bwd_attn(c + 1, second)
-
-        @pl.when(i < n)
-        def _():
-            bwd_mid(c, first, lax.rem(i, 2))
-
-        @pl.when(i >= 1)
-        def _():
-            bwd_end(c + 1, second, lax.rem(i + 1, 2))
-
-        return carry
-
-    lax.fori_loop(0, n + 1, bwd_body, 0)
+    pipeline(
+        [(bwd_mlp, 0, "bwd_mlp"), (bwd_attn, 1, "bwd_attn"), (bwd_mid, 0, "bwd_mid"), (bwd_end, 1, "bwd_end")],
+        lambda j: n - 1 - j,
+    )
 
     fin_s[...] = jnp.zeros_like(fin_s)
     fin_s[0:1, :] = jnp.sum(gacc[0], axis=0, keepdims=True)
@@ -512,8 +564,9 @@
     for d in order:
         fin_copy(d, lax.rem(me + d, n_model)).start()
 
-    rs_drain(2)
-    rs_drain(3)
+    for c in range(min(n, 2)):
+        rs_drain(2, c)
+        rs_drain(3, c)
     ag_drain(1, dmidbuf)
     staged_out(3, 0).wait()
     staged_out(4, 0).wait()
@@ -558,6 +611,10 @@
         pltpu.VMEM((hw, d_model), BF16),
         pltpu.VMEM((d_model, ff), BF16),
         pltpu.VMEM((ff, d_model), BF16),
+        pltpu.VMEM((3 * hw, d_model), BF16),
+        pltpu.VMEM((d_model, hw), BF16),
+        pltpu.VMEM((ff, d_model), BF16),
+        pltpu.VMEM((d_model, ff), BF16),
         pltpu.VMEM((seq, d_model), BF16),
         pltpu.VMEM((seq, d_model), BF16),
         pltpu.VMEM((seq, d_model), BF16),
@@ -568,8 +625,8 @@
         pltpu.VMEM((n, tq, d_model), BF16),
         pltpu.VMEM((seq, hw), F32),
         pltpu.VMEM((seq, hw), F32),
-        pltpu.VMEM((4, n, near, tq, d_model), BF16),
-        pltpu.VMEM((4, t, d_model), BF16),
+        pltpu.VMEM((2, n, near, tq, d_model), BF16),
+        pltpu.VMEM((4, 2, t, d_model), BF16),
         pltpu.VMEM((t, d_model), BF16),
         pltpu.VMEM((t, ff), BF16),
         pltpu.VMEM((t, hw), BF16),
@@ -577,13 +634,13 @@
         pltpu.VMEM((t, 3 * hw), BF16),
         pltpu.VMEM((tq, d_model), BF16),
         pltpu.VMEM((tq, d_model), BF16),
-        pltpu.VMEM((2, tq, d_model), F32),
+        pltpu.VMEM((4, tq, d_model), F32),
         pltpu.VMEM((8, d_model), F32),
         pltpu.VMEM((2, 8, d_model), F32),
         pltpu.VMEM((8, 128), F32),
         pltpu.VMEM((8, d_model), F32),
         pltpu.VMEM((near, 8, d_model), F32),
-        dma((4,)),
+        dma((3 * cfg["heads"] + 3,)),
         dma((n,)),
         dma((n,)),
         dma((n, n_model)),
@@ -591,7 +648,7 @@
         dma((n, n_model)),
         dma((n_model,)),
         dma((4, n, near)),
-        dma((4, near)),
+        dma((4, 2, near)),
         dma((2, n, near)),
         dma((2, near)),
         dma((5,)),
@@ -616,6 +673,83 @@
     )(x, y, wqkv, wout, wup, wdown, gain)
 
 
+def grads_kernel(nj, bm, *refs):
+    ins, small = refs[: 2 * nj], refs[2 * nj]
+    outs, loss_ref, gain_ref = refs[2 * nj + 1 : 3 * nj + 1], refs[3 * nj + 1], refs[3 * nj + 2]
+    scratch = refs[3 * nj + 3 :]
+    bufs, stages, in_sem, out_sem = scratch[: 2 * nj], scratch[2 * nj : 3 * nj], scratch[-2], scratch[-1]
+
+    def load(k):
+        return pltpu.make_async_copy(ins[k], bufs[k], in_sem.at[k])
+
+    for k in range(2 * nj):
+        load(k).start()
+    loss_ref[...] = small[2:3, 0:1]
+    gain_ref[...] = small[0:2, :]
+    for j in range(nj):
+        load(2 * j).wait()
+        load(2 * j + 1).wait()
+        a, b, out, stage = bufs[2 * j], bufs[2 * j + 1], outs[j], stages[j]
+        rows = a.shape[1]
+        step = min(bm, rows)
+        blocks = rows // step
+
+        def put(i, slot):
+            where = pl.ds(pl.multiple_of(i * step, step), step)
+            dst = out.at[:, where] if len(out.shape) == 3 else out.at[where]
+            return pltpu.make_async_copy(stage.at[slot], dst, out_sem.at[j, slot])
+
+        def block(i, carry):
+            slot = lax.rem(i, 2)
+
+            @pl.when(i >= 2)
+            def _():
+                put(i, slot).wait()
+
+            acc = dot_tn(a[:, pl.ds(pl.multiple_of(i * step, step), step)], b[...])
+            if len(out.shape) == 3:
+                lanes = out.shape[2]
+                for s in range(out.shape[0]):
+                    stage[slot, s] = acc[:, s * lanes : (s + 1) * lanes]
+            else:
+                stage[slot] = acc
+            put(i, slot).start()
+            return carry
+
+        lax.fori_loop(0, blocks, block, 0)
+    for j in range(nj):
+        rows = bufs[2 * j].shape[1]
+        step = min(bm, rows)
+        for slot in range(min(2, rows // step)):
+            out, stage = outs[j], stages[j]
+            dst = out.at[:, 0:step] if len(out.shape) == 3 else out.at[0:step]
+            pltpu.make_async_copy(stage.at[slot], dst, out_sem.at[j, slot]).wait()
+
+
+def weight_grads(pairs, out_shapes, small, bm):
+    nj = len(pairs)
+    flat = [x for pair in pairs for x in pair]
+    any_spec = pl.BlockSpec(memory_space=pl.ANY)
+    vmem_spec = pl.BlockSpec(memory_space=pltpu.VMEM)
+    stages = []
+    for (a, _), out in zip(pairs, out_shapes):
+        step = min(bm, a.shape[1])
+        stages.append(pltpu.VMEM((2,) + out[:-2] + (step, out[-1]), F32))
+    outs = [jax.ShapeDtypeStruct(out, F32) for out in out_shapes]
+    outs += [jax.ShapeDtypeStruct((1, 1), F32), jax.ShapeDtypeStruct((2, small.shape[1]), F32)]
+    return pl.pallas_call(
+        functools.partial(grads_kernel, nj, bm),
+        name="weight_grads",
+        out_shape=outs,
+        in_specs=[any_spec] * (2 * nj) + [vmem_spec],
+        out_specs=[any_spec] * nj + [vmem_spec] * 2,
+        scratch_shapes=[pltpu.VMEM(x.shape, x.dtype) for x in flat]
+        + stages
+        + [pltpu.SemaphoreType.DMA((2 * nj,)), pltpu.SemaphoreType.DMA((nj, 2))],
+        compiler_params=pltpu.CompilerParams(vmem_limit_bytes=VMEM_BYTES),
+    )(*flat, small)
+
+
 def solution(mesh):
     n_stage = mesh.shape["stage"]
     n_model = mesh.shape["model"]
@@ -629,14 +763,17 @@
             heads=heads, hd=hd, ff=ff, elem_count=n_batch * seq_len * d_model,
         )
         na, nb, at, z, dqkv, dmid, dup, dout, small = run_step(
-            cfg, x_in[0], y_target[0], w_qkv[0].reshape(d_model, 3 * heads * hd), w_out[0].reshape(heads * hd, d_model),
-            w_up[0], w_down[0], norm_gain[0].astype(F32),
-        )
-        grad_qkv = dot_tn(na, dqkv).reshape(1, d_model, 3, heads, hd)
-        grad_out = dot_tn(at, dmid).reshape(1, heads, hd, d_model)
-        grad_up = dot_tn(nb, dup)[None]
-        grad_down = dot_tn(z, dout)[None]
-        return small[2:3, 0], grad_qkv, grad_out, grad_up, grad_down, small[None, 0:2]
+            cfg, x_in[0], y_target[0], w_qkv[0].transpose(1, 2, 0, 3).reshape(3 * heads, d_model, hd), w_out[0].reshape(heads * hd, d_model),
+            w_up[0], w_down[0], norm_gain[0],
+        )
+        g_out, g_up, g_down, g_qkv, loss, g_gain = weight_grads(
+            [(at, dmid), (nb, dup), (z, dout), (na, dqkv)],
+            [(heads * hd, d_model), (d_model, ff), (ff, d_model), (3 * heads, d_model, hd)],
+            small,
+            tile_of(d_model, GRAD_ROWS),
+        )
+        grad_qkv = g_qkv.reshape(3, heads, d_model, hd).transpose(2, 0, 1, 3)[None]
+        return loss.reshape(1), grad_qkv, g_out.reshape(1, heads, hd, d_model), g_up[None], g_down[None], g_gain[None]
 
     act_spec = P("data", None, None)
     weight_specs = (

time: 866 us -> 703 us (0.81)
  Pallas kernels: 816 us -> 702 us
  matrix products: 28.9 us -> 0 us
  local copies, waits for them, and re-layouts: 18.7 us -> 0 us
    pallas_call x1, Pallas kernels: 816 us -> 680 us  [run_step(): pl.pallas_call(functools.partial(step_kernel, cfg), name='pipeline_step',...]
    dot_general x4 -> x0, matrix products: 28.9 us -> none  [dot_tn(): lax.dot_general(a, b, (((0,), (0,)), ((), ())), preferred_element_type=F32)]
    pallas_call x0 -> x1, Pallas kernels: none -> 22.4 us  [weight_grads(): pl.pallas_call(functools.partial(grads_kernel, nj, bm), name='weight_grad...]
    unnamed x12 -> x0, local copies, waits for them, and re-layouts: 12.5 us -> none
where the time goes in v2:
time: 703 us
  Pallas kernels  702 us (100%)
    pallas_call x1, Pallas kernels, run_step(): pl.pallas_call(functools.partial(step_kernel, cfg), name='pipeline_step',...  680 us
    pallas_call x1, Pallas kernels, weight_grads(): pl.pallas_call(functools.partial(grads_kernel, nj, bm), name='weight_grad...  22.4 us

profile of v2, /device:TPU:96, one launch (start us, length us, event | category | flops | bytes accessed | tf_op | source)
XLA Modules:
  0.0 702.9 jit_solution(9358045630135425348)
XLA Ops:
  0.6 679.7 %pipeline_step.1 = (bf16[1024,1536]{1,0:T(8,128)(2,1)}, bf16[1024,1536]{1,0:T(8,128)(2,1)}, bf16[1024,384]{1,0:T(8,128)(2,1)}, bf16[1024,1536]{1,0:T(8,128)(2,1)...) custom-call(bf16[1024,1536]{1,0:T(8,128)(2,1)} %bitcast.24, ...), custom_call_target="tpu_custom_call" | custom-call | tf_op jit(solution)/shard_map/pipeline_step/pallas_call | solution.py:660
  680.4 22.4 %weight_grads.1 = (f32[384,1536]{1,0:T(8,128)}, f32[1536,1536]{1,0:T(8,128)}, f32[1536,1536]{1,0:T(8,128)}, f32[9,1536,128]{2,1,0:T(8,128)}, f32[1,1]{1,0:T(1,128)}, /*index=5*/f32[2,1536]{1,0:T(2,128)}) custom-call(bf16[1024,384]{1,0:T(8,128)(2,1)} %get-tuple-element.21.refs_0_, bf16[1024,1536]{1,0:T(8,128)(2,1)} %get-tuple-element.22.refs_1_, ...), custom_call_target="tpu_custom_call" | custom-call | tf_op jit(solution)/shard_map/weight_grads/pallas_call | solution.py:740

commit v3 on v2

--- a/solution.py
+++ b/solution.py
@@ -71,7 +71,7 @@
         x_hbm, y_hbm, wqkv_hbm, wout_hbm, wup_hbm, wdown_hbm, gain_ref,
         na_hbm, nb_hbm, at_hbm, z_hbm, dqkv_hbm, dmid_hbm, dup_hbm, dout_hbm, small_ref,
         wqkv, wout, wup, wdown, wqkv_t, wout_t, wup_t, wdown_t, hbuf, nbbuf, doutbuf, dmidbuf, qkvbuf, upbuf, midq, yq, dkacc, dvacc,
-        rs_r, rs_s, na_st, z_st, at_st, dup_st, dqkv_st, hsend, dsend, dmidq,
+        rs_r, rs_s, na_st, z_st, at_st, dup_st, dqkv_st, ds_st, pr_st, hsend, dsend, dmidq,
         lossacc, gacc, lossbuf, fin_s, fin_r,
         w_sem, x_sem, y_sem, h_rsem, h_ssem, d_rsem, d_ssem, rs_rsem, rs_ssem, ag_rsem, ag_ssem,
         out_sem, full_sem, loss_sem, fin_rsem, fin_ssem,
@@ -81,6 +81,11 @@
     last = n_stage - 1
     order = [d for d in (2, 1, 3) if d < n_model] if n_model > 2 else list(range(1, n_model))
 
+    odd = lax.rem(me, 2)
+    send_order = [2, 3 - 2 * odd, 1 + 2 * odd] if n_model == 4 else order
+
+    far_first = [2, 3 - 2 * odd, 1 + 2 * odd, 0] if n_model == 4 else list(range(n_model))
+
     def remote(src, dst, ssem, rsem, where):
         return pltpu.make_async_remote_copy(
             src_ref=src, dst_ref=dst, send_sem=ssem, recv_sem=rsem, device_id=where, device_id_type=MESH_ID
@@ -103,11 +108,15 @@
         dst = (wout, wup, wdown)[k - slabs]
         return pltpu.make_async_copy(src, dst, w_sem.at[k])
 
-    def x_copy(c):
-        return pltpu.make_async_copy(x_hbm.at[rows_of(c)], hbuf.at[rows_of(c)], x_sem.at[c])
+    def x_copy(k):
+        rows = pl.ds(0, t) if k == 0 else pl.ds(t, seq - t)
+        return pltpu.make_async_copy(x_hbm.at[rows], hbuf.at[rows], x_sem.at[k])
 
     def y_copy(c):
-        return pltpu.make_async_copy(y_hbm.at[quarter(c, me)], yq.at[c], y_sem.at[c])
+        return pltpu.make_async_copy(y_hbm.at[quarter(c, me)], yq.at[pl.ds(c * tq, tq)], y_sem.at[0])
+
+    def y_all():
+        return pltpu.make_async_copy(y_hbm.at[pl.ds(0, n * tq)], yq, y_sem.at[0])
 
     @pl.when(stage == 0)
     def _():
@@ -118,8 +127,7 @@
 
     @pl.when(stage == 0)
     def _():
-        for c in range(1, n):
-            x_copy(c).start()
+        x_copy(1).start()
 
     @pl.when(stage == last)
     def _():
@@ -145,65 +153,79 @@
     gain_a = gains[0:1, :]
     gain_b = gains[1:2, :]
 
+    others = n_model - 1
+
     def rs_copy(p, c, d, peer):
         slot = lax.rem(c, 2)
         return remote(
-            rs_s.at[p, slot, pl.ds(pl.multiple_of(peer * tq, tq), tq)], rs_r.at[p % 2, c, d - 1],
-            rs_ssem.at[p, slot, d - 1], rs_rsem.at[p, c, d - 1], {"model": peer},
+            rs_s.at[p, slot, pl.ds(pl.multiple_of(peer * tq, tq), tq)], rs_r.at[p, slot, d - 1],
+            rs_ssem.at[p, slot], rs_rsem.at[p, slot], {"model": peer},
         )
 
+    def rs_all(p, c):
+        slot = lax.rem(c, 2)
+        return remote(rs_r.at[p, slot], rs_r.at[p, slot], rs_ssem.at[p, slot], rs_rsem.at[p, slot], {"model": 0})
+
     def rs_start(p, c):
-        for d in order:
+        for d in send_order:
             rs_copy(p, c, d, lax.rem(me + d, n_model)).start()
 
     def rs_drain(p, c):
-        for d in order:
-            rs_copy(p, c, d, 0).wait_send()
+        rs_all(p, c).wait_send()
 
     def rs_sum(p, c):
         with jax.named_scope(f"rs_wait{p}"):
-            for d in order:
-                rs_copy(p, c, d, 0).wait_recv()
+            rs_all(p, c).wait_recv()
         total = rs_s[p, lax.rem(c, 2), own, :].astype(F32)
         for d in range(1, n_model):
-            total = total + rs_r[p % 2, c, d - 1].astype(F32)
+            total = total + rs_r[p, lax.rem(c, 2), d - 1].astype(F32)
         return total
 
-    def ag_copy(p, buf, c, d, peer, owner):
+    def ag_copy(p, buf, c, peer):
+        slot = lax.rem(c, 2)
         return remote(
-            buf.at[quarter(c, owner)], buf.at[quarter(c, owner)],
-            ag_ssem.at[p, d - 1], ag_rsem.at[p, c, d - 1], {"model": peer},
+            buf.at[quarter(c, me)], buf.at[quarter(c, me)], ag_ssem.at[p], ag_rsem.at[p, slot], {"model": peer}
         )
 
+    def ag_all(p, buf, c):
+        rows = pl.ds(0, others * tq)
+        return remote(buf.at[rows], buf.at[rows], ag_ssem.at[p], ag_rsem.at[p, lax.rem(c, 2)], {"model": 0})
+
     def ag_start(p, buf, c):
-        for d in order:
-            ag_copy(p, buf, c, d, lax.rem(me + d, n_model), me).start()
+        for d in send_order:
+            ag_copy(p, buf, c, lax.rem(me + d, n_model)).start()
 
     def ag_drain(p, buf):
-        for d in order:
-            ag_copy(p, buf, 0, d, 0, 0).wait_send()
+        ag_all(p, buf, 0).wait_send()
 
     def ag_wait(p, buf, c):
         with jax.named_scope(f"ag_wait{p}"):
-            for d in order:
-                ag_copy(p, buf, c, d, 0, lax.rem(me + n_model - d, n_model)).wait_recv()
-
-    def h_copy(c, m, sender):
+            ag_all(p, buf, c).wait_recv()
+
+    def h_copy(c, m):
         return remote(
-            hsend, hbuf.at[quarter(c, sender)], h_ssem.at[m], h_rsem.at[c, sender], {"stage": up_stage, "model": m}
+            hsend, hbuf.at[quarter(c, me)], h_ssem.at[0], h_rsem.at[c], {"stage": up_stage, "model": m}
         )
 
-    def d_copy(c, m, sender):
+    def h_all(c):
+        return remote(hbuf.at[rows_of(c)], hbuf.at[rows_of(c)], h_ssem.at[0], h_rsem.at[c], {"model": 0})
+
+    def d_copy(c, m):
         return remote(
-            dsend, doutbuf.at[quarter(c, sender)], d_ssem.at[m], d_rsem.at[c, sender],
-            {"stage": down_stage, "model": m},
+            dsend, doutbuf.at[quarter(c, me)], d_ssem.at[0], d_rsem.at[c], {"stage": down_stage, "model": m}
         )
 
-    def peer_d_copy(c, d, peer, sender):
+    def d_all(c):
+        return remote(doutbuf.at[rows_of(c)], doutbuf.at[rows_of(c)], d_ssem.at[0], d_rsem.at[c], {"model": 0})
+
+    def peer_d_copy(c, peer):
         return remote(
-            doutbuf.at[quarter(c, sender)], doutbuf.at[quarter(c, sender)], d_ssem.at[d], d_rsem.at[c, sender],
-            {"model": peer},
+            doutbuf.at[quarter(c, me)], doutbuf.at[quarter(c, me)], d_ssem.at[0], d_rsem.at[c], {"model": peer}
         )
+
+    def peer_d_all(c):
+        rows = pl.ds(0, others * tq)
+        return remote(doutbuf.at[rows], doutbuf.at[rows], d_ssem.at[0], d_rsem.at[c], {"model": 0})
 
     def staged_out(k, c):
         src = (na_st, z_st, at_st, dup_st, dqkv_st)[k]
@@ -213,9 +235,13 @@
     def full_out(k, c):
         src = (nbbuf, dmidbuf, doutbuf)[k]
         dst = (nb_hbm, dmid_hbm, dout_hbm)[k]
-        return pltpu.make_async_copy(src.at[rows_of(c)], dst.at[rows_of(c)], full_sem.at[k, c])
+        return pltpu.make_async_copy(src.at[rows_of(c)], dst.at[rows_of(c)], full_sem.at[k])
+
+    def full_all(k):
+        return pltpu.make_async_copy((nbbuf, dmidbuf, doutbuf)[k], (nb_hbm, dmid_hbm, dout_hbm)[k], full_sem.at[k])
 
     key_step = min(KEY_STEP, seq)
+    key_block = max(t, 128)
 
     def by_prefix(c, body):
         need = lax.div(c * t + t - 1, key_step)
@@ -239,15 +265,18 @@
         return e * (1.0 / jnp.sum(e, axis=-1, keepdims=True))
 
     def fwd_attn(c, first):
-        @pl.when(stage == 0)
-        def _():
-            x_copy(c).wait()
+        @pl.when(first & (stage == 0))
+        def _():
+            x_copy(0).wait()
+
+        @pl.when((c == 1) & (stage == 0))
+        def _():
+            x_copy(1).wait()
 
         @pl.when(stage > 0)
         def _():
             with jax.named_scope("h_wait"):
-                for m in range(n_model):
-                    h_copy(c, 0, m).wait_recv()
+                h_all(c).wait_recv()
 
         @pl.when(first & (stage == 0))
         def _():
@@ -336,27 +365,27 @@
         def _():
             @pl.when(jnp.logical_not(first))
             def _():
-                for m in range(n_model):
-                    h_copy(c, m, me).wait_send()
+                h_all(c).wait_send()
 
             hsend[...] = h_out
-            for m in range(n_model):
-                h_copy(c, m, me).start()
+            for d in far_first:
+                h_copy(c, lax.rem(me + d, n_model)).start()
 
         @pl.when(stage == last)
         def _():
-            y_copy(c).wait()
+            @pl.when(first)
+            def _():
+                y_all().wait()
 
             @pl.when(jnp.logical_not(first))
             def _():
-                for d in order:
-                    peer_d_copy(c, d, 0, me).wait_send()
-
-            diff = h_out.astype(F32) - yq[c].astype(F32)
+                peer_d_all(c).wait_send()
+
+            diff = h_out.astype(F32) - yq[pl.ds(pl.multiple_of(c * tq, tq), tq), :].astype(F32)
             lossacc[...] += fold_rows(diff * diff)
             doutbuf[quarter(c, me), :] = (diff * (1.0 / elem_count)).astype(BF16)
             for d in order:
-                peer_d_copy(c, d, lax.rem(me + d, n_model), me).start()
+                peer_d_copy(c, lax.rem(me + d, n_model)).start()
 
     def pipeline(phases, chunk_of):
         deepest = max(lag for _, lag, _ in phases)
@@ -408,13 +437,11 @@
 
     @pl.when(stage < last)
     def _():
-        for m in range(n_model):
-            h_copy(0, m, me).wait_send()
+        h_all(0).wait_send()
 
     @pl.when(stage == last)
     def _():
-        for d in order:
-            peer_d_copy(0, d, 0, me).wait_send()
+        peer_d_all(0).wait_send()
         total = lossacc[:, 0:128]
         for j in range(1, d_model // 128):
             total = total + lossacc[:, j * 128 : (j + 1) * 128]
@@ -431,13 +458,11 @@
         @pl.when(stage < last)
         def _():
             with jax.named_scope("d_wait"):
-                for m in range(n_model):
-                    d_copy(c, 0, m).wait_recv()
+                d_all(c).wait_recv()
 
         @pl.when(stage == last)
         def _():
-            for d in order:
-                peer_d_copy(c, d, 0, lax.rem(me + n_model - d, n_model)).wait_recv()
+            peer_d_all(c).wait_recv()
 
         full_out(2, c).start()
 
@@ -482,7 +507,7 @@
         def _():
             staged_out(4, c).wait()
 
-        @pl.when(c < n - 2)
+        @pl.when((c < n - 2) & (stage > 0))
         def _():
             rs_drain(3, c)
 
@@ -504,39 +529,64 @@
                 d_scores.append((p * (dp - jnp.sum(p * dp, axis=-1, keepdims=True)) * scale).astype(BF16))
             for i in range(heads):
                 cols = slice(i * hd, (i + 1) * hd)
+                ds_st[i, :, 0:keys] = d_scores[i]
+                pr_st[i, :, 0:keys] = probs[i]
                 dqkv_st[:, cols] = dot_nn(d_scores[i], qkvbuf[0:keys, hw + i * hd : hw + (i + 1) * hd]).astype(BF16)
-            for i in range(heads):
-                cols = slice(i * hd, (i + 1) * hd)
-                dkacc[0:keys, cols] += dot_tn(d_scores[i], qkvbuf[rows_of(c), cols])
-                dvacc[0:keys, cols] += dot_tn(probs[i], at_st[:, cols])
 
         by_prefix(c, attend)
+        near_keys = pl.ds(pl.multiple_of(lax.div(c * t, key_block) * key_block, key_block), key_block)
+        for i in range(heads):
+            cols = slice(i * hd, (i + 1) * hd)
+            dkacc[near_keys, cols] += dot_tn(ds_st[i, :, near_keys], qkvbuf[rows_of(c), cols])
+            dvacc[near_keys, cols] += dot_tn(pr_st[i, :, near_keys], at_st[:, cols])
         dqkv_st[:, hw : 2 * hw] = dkacc[rows_of(c), :].astype(BF16)
         dqkv_st[:, 2 * hw : 3 * hw] = dvacc[rows_of(c), :].astype(BF16)
         staged_out(4, c).start()
         tile = tile_of(d_model)
-        for j in range(d_model // tile):
-            cols = slice(j * tile, (j + 1) * tile)
-            rs_s[3, slot, :, cols] = dot_nn(dqkv_st[...], wqkv_t[:, cols]).astype(BF16)
-        rs_start(3, c)
+
+        @pl.when(stage > 0)
+        def _():
+            for j in range(d_model // tile):
+                cols = slice(j * tile, (j + 1) * tile)
+                rs_s[3, slot, :, cols] = dot_nn(dqkv_st[...], wqkv_t[:, cols]).astype(BF16)
+            rs_start(3, c)
+
+        @pl.when(stage == 0)
+        def _():
+            h32 = hbuf[rows_of(c), :].astype(F32)
+            normed = h32 * rms_inverse(h32)
+            for j in range(d_model // tile):
+                cols = slice(j * tile, (j + 1) * tile)
+                gacc[0, :, cols] += fold_rows(dot_nn(dqkv_st[...], wqkv_t[:, cols]) * normed[:, cols])
+
+        def older(keys):
+            for i in range(heads):
+                cols = slice(i * hd, (i + 1) * hd)
+                ds_st[i, :, near_keys] = jnp.zeros((t, key_block), BF16)
+                pr_st[i, :, near_keys] = jnp.zeros((t, key_block), BF16)
+            for i in range(heads):
+                cols = slice(i * hd, (i + 1) * hd)
+                dkacc[0:keys, cols] += dot_tn(ds_st[i, :, 0:keys], qkvbuf[rows_of(c), cols])
+                dvacc[0:keys, cols] += dot_tn(pr_st[i, :, 0:keys], at_st[:, cols])
+
+        by_prefix(c, older)
 
     def loss_copy():
         return remote(lossbuf, lossbuf, loss_sem.at[0], loss_sem.at[1], {"stage": down_stage})
 
     def bwd_end(c, first):
-        h32 = hbuf[quarter(c, me), :].astype(F32)
-        d_in = dmidq[lax.rem(c, 4)] + rms_backward(h32, gain_a, rs_sum(3, c), 0)
-
         @pl.when(stage > 0)
         def _():
+            h32 = hbuf[quarter(c, me), :].astype(F32)
+            d_in = dmidq[lax.rem(c, 4)] + rms_backward(h32, gain_a, rs_sum(3, c), 0)
+
             @pl.when(jnp.logical_not(first))
             def _():
-                for m in range(n_model):
-                    d_copy(c, m, me).wait_send()
+                d_all(c).wait_send()
 
             dsend[...] = d_in.astype(BF16)
-            for m in range(n_model):
-                d_copy(c, m, me).start()
+            for d in far_first:
+                d_copy(c, lax.rem(me + d, n_model)).start()
 
         @pl.when(first)
         def _():
@@ -559,29 +609,28 @@
     fin_s[2:3, 0:128] = jnp.sum(lossbuf[...], axis=0, keepdims=True)
 
     def fin_copy(d, peer):
-        return remote(fin_s, fin_r.at[d - 1], fin_ssem.at[d - 1], fin_rsem.at[d - 1], {"model": peer})
+        return remote(fin_s, fin_r.at[d - 1], fin_ssem.at[0], fin_rsem.at[0], {"model": peer})
 
     for d in order:
         fin_copy(d, lax.rem(me + d, n_model)).start()
 
     for c in range(min(n, 2)):
         rs_drain(2, c)
-        rs_drain(3, c)
     ag_drain(1, dmidbuf)
     staged_out(3, 0).wait()
     staged_out(4, 0).wait()
     for k in range(3):
-        for c in range(n):
-            full_out(k, c).wait()
+        full_all(k).wait()
 
     @pl.when(stage > 0)
     def _():
-        for m in range(n_model):
-            d_copy(0, m, me).wait_send()
+        for c in range(min(n, 2)):
+            rs_drain(3, c)
+        d_all(0).wait_send()
         loss_copy().wait_send()
 
-    for d in order:
-        fin_copy(d, 0).wait_recv()
+    fin_all = remote(fin_r, fin_r, fin_ssem.at[0], fin_rsem.at[0], {"model": 0})
+    fin_all.wait_recv()
     parts = [jnp.where(me == 0, fin_s[...], 0.0)]
     for m in range(n_model):
         term = jnp.where(me == m, fin_s[...], 0.0)
@@ -594,8 +643,7 @@
     small_ref[0:2, :] = total[0:2, :]
     loss = jnp.sum(total[2:3, :], axis=-1, keepdims=True) * (0.5 / elem_count)
     small_ref[2:8, :] = jnp.broadcast_to(loss, (6, d_model))
-    for d in order:
-        fin_copy(d, 0).wait_send()
+    fin_all.wait_send()
 
 
 def run_step(cfg, x, y, wqkv, wout, wup, wdown, gain):
@@ -622,16 +670,18 @@
         pltpu.VMEM((seq, 3 * hw), BF16),
         pltpu.VMEM((seq, ff), F32),
         pltpu.VMEM((n, tq, d_model), F32),
-        pltpu.VMEM((n, tq, d_model), BF16),
+        pltpu.VMEM((n * tq, d_model), BF16),
         pltpu.VMEM((seq, hw), F32),
         pltpu.VMEM((seq, hw), F32),
-        pltpu.VMEM((2, n, near, tq, d_model), BF16),
+        pltpu.VMEM((4, 2, near, tq, d_model), BF16),
         pltpu.VMEM((4, 2, t, d_model), BF16),
         pltpu.VMEM((t, d_model), BF16),
         pltpu.VMEM((t, ff), BF16),
         pltpu.VMEM((t, hw), BF16),
         pltpu.VMEM((t, ff), BF16),
         pltpu.VMEM((t, 3 * hw), BF16),
+        pltpu.VMEM((cfg["heads"], t, seq), BF16),
+        pltpu.VMEM((cfg["heads"], t, seq), BF16),
         pltpu.VMEM((tq, d_model), BF16),
         pltpu.VMEM((tq, d_model), BF16),
         pltpu.VMEM((4, tq, d_model), F32),
@@ -641,21 +691,21 @@
         pltpu.VMEM((8, d_model), F32),
         pltpu.VMEM((near, 8, d_model), F32),
         dma((3 * cfg["heads"] + 3,)),
+        dma((2,)),
+        dma((1,)),
         dma((n,)),
+        dma((1,)),
         dma((n,)),
-        dma((n, n_model)),
-        dma((n_model,)),
-        dma((n, n_model)),
-        dma((n_model,)),
-        dma((4, n, near)),
-        dma((4, 2, near)),
-        dma((2, n, near)),
-        dma((2, near)),
+        dma((1,)),
+        dma((4, 2)),
+        dma((4, 2)),
+        dma((2, 2)),
+        dma((2,)),
         dma((5,)),
-        dma((3, n)),
+        dma((3,)),
         dma((2,)),
-        dma((near,)),
-        dma((near,)),
+        dma((1,)),
+        dma((1,)),
     ]
     return pl.pallas_call(
         functools.partial(step_kernel, cfg),

time: 703 us -> 673 us (0.957)
  Pallas kernels: 702 us -> 672 us
    pallas_call x1, Pallas kernels: 680 us -> 649 us  [run_step(): pl.pallas_call(functools.partial(step_kernel, cfg), name='pipeline_step',...]
where the time goes in v3:
time: 673 us
  Pallas kernels  672 us (100%)
    pallas_call x1, Pallas kernels, run_step(): pl.pallas_call(functools.partial(step_kernel, cfg), name='pipeline_step',...  649 us
    pallas_call x1, Pallas kernels, weight_grads(): pl.pallas_call(functools.partial(grads_kernel, nj, bm), name='weight_grad...  22.4 us

profile of v3, /device:TPU:96, one launch (start us, length us, event | category | flops | bytes accessed | tf_op | source)
XLA Modules:
  0.0 672.5 jit_solution(11454728081578295914)
XLA Ops:
  0.6 649.3 %pipeline_step.1 = (bf16[1024,1536]{1,0:T(8,128)(2,1)}, bf16[1024,1536]{1,0:T(8,128)(2,1)}, bf16[1024,384]{1,0:T(8,128)(2,1)}, bf16[1024,1536]{1,0:T(8,128)(2,1)...) custom-call(bf16[1024,1536]{1,0:T(8,128)(2,1)} %bitcast.24, ...), custom_call_target="tpu_custom_call" | custom-call | tf_op jit(solution)/shard_map/pipeline_step/pallas_call | solution.py:710
  650.0 22.4 %weight_grads.1 = (f32[384,1536]{1,0:T(8,128)}, f32[1536,1536]{1,0:T(8,128)}, f32[1536,1536]{1,0:T(8,128)}, f32[9,1536,128]{2,1,0:T(8,128)}, f32[1,1]{1,0:T(1,128)}, /*index=5*/f32[2,1536]{1,0:T(2,128)}) custom-call(bf16[1024,384]{1,0:T(8,128)(2,1)} %get-tuple-element.21.refs_0_, bf16[1024,1536]{1,0:T(8,128)(2,1)} %get-tuple-element.22.refs_1_, ...), custom_call_target="tpu_custom_call" | custom-call | tf_op jit(solution)/shard_map/weight_grads/pallas_call | solution.py:790

commit v4 on v3

--- a/solution.py
+++ b/solution.py
@@ -69,7 +69,7 @@
     scale = hd**-0.5
     (
         x_hbm, y_hbm, wqkv_hbm, wout_hbm, wup_hbm, wdown_hbm, gain_ref,
-        na_hbm, nb_hbm, at_hbm, z_hbm, dqkv_hbm, dmid_hbm, dup_hbm, dout_hbm, small_ref,
+        na_hbm, nb_hbm, at_hbm, z_hbm, dqkv_hbm, dmid_hbm, dup_hbm, dout_hbm, small_hbm,
         wqkv, wout, wup, wdown, wqkv_t, wout_t, wup_t, wdown_t, hbuf, nbbuf, doutbuf, dmidbuf, qkvbuf, upbuf, midq, yq, dkacc, dvacc,
         rs_r, rs_s, na_st, z_st, at_st, dup_st, dqkv_st, ds_st, pr_st, hsend, dsend, dmidq,
         lossacc, gacc, lossbuf, fin_s, fin_r,
@@ -388,13 +388,16 @@
                 peer_d_copy(c, lax.rem(me + d, n_model)).start()
 
     def pipeline(phases, chunk_of):
-        deepest = max(lag for _, lag, _ in phases)
+        deepest = max(p[1] for p in phases)
 
         def body(i, carry):
-            for phase, lag, name in phases:
+            for phase, lag, name, *cond in phases:
                 j = i - lag
-
-                @pl.when((j >= 0) & (j < n))
+                ok = (j >= 0) & (j < n)
+                if cond:
+                    ok = ok & cond[0]
+
+                @pl.when(ok)
                 def _():
                     with jax.named_scope(name):
                         phase(chunk_of(j), j == 0)
@@ -416,7 +419,7 @@
         flip_weights()
 
     pipeline(
-        [(fwd_attn, 0, "fwd_attn"), (fwd_mlp, 1, "fwd_mlp"), (fwd_mid, 0, "fwd_mid"), (fwd_end, 1, "fwd_end")],
+        [(fwd_attn, 0, "fwd_attn"), (fwd_end, 2, "fwd_end", lax.rem(stage, 2) == 0), (fwd_mlp, 1, "fwd_mlp"), (fwd_mid, 0, "fwd_mid"), (fwd_end, 1, "fwd_end", lax.rem(stage, 2) == 1)],
         lambda j: j,
     )
 
@@ -447,12 +450,14 @@
             total = total + lossacc[:, j * 128 : (j + 1) * 128]
         lossbuf[...] = total
 
-    def rms_backward(v, gain, d_norm, k):
+    def rms_backward(v, gain, k, d_norm_of):
         inv = rms_inverse(v)
         normed = v * inv
+        scaled = gain * inv
+        d_norm = d_norm_of()
         gacc[k] += fold_rows(d_norm * normed)
         d_normed = d_norm * gain
-        return inv * (d_normed - normed * jnp.mean(d_normed * normed, axis=-1, keepdims=True))
+        return d_norm * scaled - normed * (inv * jnp.mean(d_normed * normed, axis=-1, keepdims=True))
 
     def bwd_mlp(c, first):
         @pl.when(stage < last)
@@ -493,8 +498,8 @@
         def _():
             ag_drain(1, dmidbuf)
 
-        d_norm = rs_sum(2, c)
-        d_mid = doutbuf[quarter(c, me), :].astype(F32) + rms_backward(midq[c], gain_b, d_norm, 1)
+        d_out = doutbuf[quarter(c, me), :].astype(F32)
+        d_mid = d_out + rms_backward(midq[c], gain_b, 1, lambda: rs_sum(2, c))
         dmidq[lax.rem(c, 4)] = d_mid
         dmidbuf[quarter(c, me), :] = d_mid.astype(BF16)
         ag_start(1, dmidbuf, c)
@@ -569,7 +574,9 @@
                 dkacc[0:keys, cols] += dot_tn(ds_st[i, :, 0:keys], qkvbuf[rows_of(c), cols])
                 dvacc[0:keys, cols] += dot_tn(pr_st[i, :, 0:keys], at_st[:, cols])
 
-        by_prefix(c, older)
+        @pl.when(c * t >= key_block)
+        def _():
+            by_prefix(c, older)
 
     def loss_copy():
         return remote(lossbuf, lossbuf, loss_sem.at[0], loss_sem.at[1], {"stage": down_stage})
@@ -578,7 +585,7 @@
         @pl.when(stage > 0)
         def _():
             h32 = hbuf[quarter(c, me), :].astype(F32)
-            d_in = dmidq[lax.rem(c, 4)] + rms_backward(h32, gain_a, rs_sum(3, c), 0)
+            d_in = dmidq[lax.rem(c, 4)] + rms_backward(h32, gain_a, 0, lambda: rs_sum(3, c))
 
             @pl.when(jnp.logical_not(first))
             def _():
@@ -599,7 +606,7 @@
                 loss_copy().start()
 
     pipeline(
-        [(bwd_mlp, 0, "bwd_mlp"), (bwd_attn, 1, "bwd_attn"), (bwd_mid, 0, "bwd_mid"), (bwd_end, 1, "bwd_end")],
+        [(bwd_mlp, 0, "bwd_mlp"), (bwd_end, 2, "bwd_end", lax.rem(stage, 2) == 0), (bwd_attn, 1, "bwd_attn"), (bwd_mid, 0, "bwd_mid"), (bwd_end, 1, "bwd_end", lax.rem(stage, 2) == 1)],
         lambda j: n - 1 - j,
     )
 
@@ -631,6 +638,7 @@
 
     fin_all = remote(fin_r, fin_r, fin_ssem.at[0], fin_rsem.at[0], {"model": 0})
     fin_all.wait_recv()
+    fin_all.wait_send()
     parts = [jnp.where(me == 0, fin_s[...], 0.0)]
     for m in range(n_model):
         term = jnp.where(me == m, fin_s[...], 0.0)
@@ -640,10 +648,12 @@
     total = parts[1]
     for m in range(1, n_model):
         total = total + parts[m + 1]
-    small_ref[0:2, :] = total[0:2, :]
+    fin_s[0:2, :] = total[0:2, :]
     loss = jnp.sum(total[2:3, :], axis=-1, keepdims=True) * (0.5 / elem_count)
-    small_ref[2:8, :] = jnp.broadcast_to(loss, (6, d_model))
-    fin_all.wait_send()
+    fin_s[2:8, :] = jnp.broadcast_to(loss, (6, d_model))
+    small_out = pltpu.make_async_copy(fin_s, small_hbm, out_sem.at[0])
+    small_out.start()
+    small_out.wait()
 
 
 def run_step(cfg, x, y, wqkv, wout, wup, wdown, gain):
@@ -715,7 +725,7 @@
             jax.ShapeDtypeStruct((8, d_model), F32),
         ),
         in_specs=[any_spec] * 6 + [vmem_spec],
-        out_specs=[any_spec] * 8 + [vmem_spec],
+        out_specs=[any_spec] * 9,
         scratch_shapes=scratch,
         compiler_params=pltpu.CompilerParams(
             collective_id=0, has_side_effects=True, vmem_limit_bytes=VMEM_BYTES
@@ -725,17 +735,18 @@
 
 def grads_kernel(nj, bm, *refs):
     ins, small = refs[: 2 * nj], refs[2 * nj]
-    outs, loss_ref, gain_ref = refs[2 * nj + 1 : 3 * nj + 1], refs[3 * nj + 1], refs[3 * nj + 2]
+    outs, loss_hbm, gain_hbm = refs[2 * nj + 1 : 3 * nj + 1], refs[3 * nj + 1], refs[3 * nj + 2]
     scratch = refs[3 * nj + 3 :]
-    bufs, stages, in_sem, out_sem = scratch[: 2 * nj], scratch[2 * nj : 3 * nj], scratch[-2], scratch[-1]
+    bufs, stages = scratch[: 2 * nj], scratch[2 * nj : 3 * nj]
+    small_buf, loss_buf, gain_buf, in_sem, out_sem, small_sem = scratch[3 * nj :]
 
     def load(k):
         return pltpu.make_async_copy(ins[k], bufs[k], in_sem.at[k])
 
     for k in range(2 * nj):
         load(k).start()
-    loss_ref[...] = small[2:3, 0:1]
-    gain_ref[...] = small[0:2, :]
+    small_in = pltpu.make_async_copy(small, small_buf, small_sem.at[0])
+    small_in.start()
     for j in range(nj):
         load(2 * j).wait()
         load(2 * j + 1).wait()
@@ -767,6 +778,13 @@
             return carry
 
         lax.fori_loop(0, blocks, block, 0)
+    small_in.wait()
+    loss_buf[...] = small_buf[2:3, 0:1]
+    gain_buf[...] = small_buf[0:2, :]
+    loss_out = pltpu.make_async_copy(loss_buf, loss_hbm, small_sem.at[0])
+    gain_out = pltpu.make_async_copy(gain_buf, gain_hbm, small_sem.at[1])
+    loss_out.start()
+    gain_out.start()
     for j in range(nj):
         rows = bufs[2 * j].shape[1]
         step = min(bm, rows)
@@ -774,13 +792,14 @@
             out, stage = outs[j], stages[j]
             dst = out.at[:, 0:step] if len(out.shape) == 3 else out.at[0:step]
             pltpu.make_async_copy(stage.at[slot], dst, out_sem.at[j, slot]).wait()
+    loss_out.wait()
+    gain_out.wait()
 
 
 def weight_grads(pairs, out_shapes, small, bm):
     nj = len(pairs)
     flat = [x for pair in pairs for x in pair]
     any_spec = pl.BlockSpec(memory_space=pl.ANY)
-    vmem_spec = pl.BlockSpec(memory_space=pltpu.VMEM)
     stages = []
     for (a, _), out in zip(pairs, out_shapes):
         step = min(bm, a.shape[1])
@@ -791,11 +810,12 @@
         functools.partial(grads_kernel, nj, bm),
         name="weight_grads",
         out_shape=outs,
-        in_specs=[any_spec] * (2 * nj) + [vmem_spec],
-        out_specs=[any_spec] * nj + [vmem_spec] * 2,
+        in_specs=[any_spec] * (2 * nj + 1),
+        out_specs=[any_spec] * (nj + 2),
         scratch_shapes=[pltpu.VMEM(x.shape, x.dtype) for x in flat]
         + stages
-        + [pltpu.SemaphoreType.DMA((2 * nj,)), pltpu.SemaphoreType.DMA((nj, 2))],
+        + [pltpu.VMEM(small.shape, F32), pltpu.VMEM((1, 1), F32), pltpu.VMEM((2, small.shape[1]), F32)]
+        + [pltpu.SemaphoreType.DMA((2 * nj,)), pltpu.SemaphoreType.DMA((nj, 2)), pltpu.SemaphoreType.DMA((2,))],
         compiler_params=pltpu.CompilerParams(vmem_limit_bytes=VMEM_BYTES),
     )(*flat, small)
 

time: 673 us -> 667 us (level)
  no operation moved by 1% of the time
where the time goes in v4:
time: 667 us
  Pallas kernels  666 us (100%)
    pallas_call x1, Pallas kernels, run_step(): pl.pallas_call(functools.partial(step_kernel, cfg), name='pipeline_step',...  645 us
    pallas_call x1, Pallas kernels, weight_grads(): pl.pallas_call(functools.partial(grads_kernel, nj, bm), name='weight_grad...  21 us

profile of v4, /device:TPU:96, one launch (start us, length us, event | category | flops | bytes accessed | tf_op | source)
XLA Modules:
  0.0 666.8 jit_solution(7270795708982305470)
XLA Ops:
  0.6 645.0 %pipeline_step.1 = (bf16[1024,1536]{1,0:T(8,128)(2,1)}, bf16[1024,1536]{1,0:T(8,128)(2,1)}, bf16[1024,384]{1,0:T(8,128)(2,1)}, bf16[1024,1536]{1,0:T(8,128)(2,1)...) custom-call(bf16[1024,1536]{1,0:T(8,128)(2,1)} %bitcast.24, ...), custom_call_target="tpu_custom_call" | custom-call | tf_op jit(solution)/shard_map/pipeline_step/pallas_call | solution.py:720
  645.6 21.0 %weight_grads.1 = (f32[384,1536]{1,0:T(8,128)}, f32[1536,1536]{1,0:T(8,128)}, f32[1536,1536]{1,0:T(8,128)}, f32[9,1536,128]{2,1,0:T(8,128)}, f32[1,1]{1,0:T(1,128)}, /*index=5*/f32[2,1536]{1,0:T(2,128)}) custom-call(bf16[1024,384]{1,0:T(8,128)(2,1)} %get-tuple-element.21.refs_0_, bf16[1024,1536]{1,0:T(8,128)(2,1)} %get-tuple-element.22.refs_1_, ...), custom_call_target="tpu_custom_call" | custom-call | tf_op jit(solution)/shard_map/weight_grads/pallas_call | solution.py:809

commit v5 on v4

--- a/solution.py
+++ b/solution.py
@@ -12,6 +12,7 @@
 NEG_BIG = -1e30
 CHUNK = 64
 KEY_STEP = 256
+SPREAD_FROM = 4
 GRAD_ROWS = 768
 LOG2E = 1.4426950408889634
 F32 = jnp.float32
@@ -71,14 +72,15 @@
         x_hbm, y_hbm, wqkv_hbm, wout_hbm, wup_hbm, wdown_hbm, gain_ref,
         na_hbm, nb_hbm, at_hbm, z_hbm, dqkv_hbm, dmid_hbm, dup_hbm, dout_hbm, small_hbm,
         wqkv, wout, wup, wdown, wqkv_t, wout_t, wup_t, wdown_t, hbuf, nbbuf, doutbuf, dmidbuf, qkvbuf, upbuf, midq, yq, dkacc, dvacc,
-        rs_r, rs_s, na_st, z_st, at_st, dup_st, dqkv_st, ds_st, pr_st, hsend, dsend, dmidq,
+        rs_r, rs_s, heads_r, na_st, z_st, at_st, dup_st, dqkv_st, ds_st, pr_st, hsend, dsend, dmidq,
         lossacc, gacc, lossbuf, fin_s, fin_r,
-        w_sem, x_sem, y_sem, h_rsem, h_ssem, d_rsem, d_ssem, rs_rsem, rs_ssem, ag_rsem, ag_ssem,
+        w_sem, x_sem, y_sem, h_rsem, h_ssem, d_rsem, d_ssem, rs_rsem, rs_ssem, ag_rsem, ag_ssem, wout_sem, heads_sem,
         out_sem, full_sem, loss_sem, fin_rsem, fin_ssem,
     ) = refs
     me = lax.axis_index("model")
     stage = lax.axis_index("stage")
     last = n_stage - 1
+    spread = stage >= SPREAD_FROM
     order = [d for d in (2, 1, 3) if d < n_model] if n_model > 2 else list(range(1, n_model))
 
     odd = lax.rem(me, 2)
@@ -98,6 +100,7 @@
         return pl.ds(pl.multiple_of(c * t + m * tq, tq), tq)
 
     own = pl.ds(pl.multiple_of(me * tq, tq), tq)
+    own_heads = pl.ds(pl.multiple_of(me * hw, hw), hw)
 
     slabs = 3 * heads
 
@@ -105,7 +108,7 @@
         if k < slabs:
             return pltpu.make_async_copy(wqkv_hbm.at[k], wqkv.at[:, pl.ds(k * hd, hd)], w_sem.at[k])
         src = (wout_hbm, wup_hbm, wdown_hbm)[k - slabs]
-        dst = (wout, wup, wdown)[k - slabs]
+        dst = (wout.at[own_heads], wup, wdown)[k - slabs]
         return pltpu.make_async_copy(src, dst, w_sem.at[k])
 
     def x_copy(k):
@@ -202,6 +205,25 @@
         with jax.named_scope(f"ag_wait{p}"):
             ag_all(p, buf, c).wait_recv()
 
+    def wout_copy(peer):
+        return remote(wout.at[own_heads], wout.at[own_heads], wout_sem.at[0], wout_sem.at[1], {"model": peer})
+
+    def wout_all():
+        rows = pl.ds(0, others * hw)
+        return remote(wout.at[rows], wout.at[rows], wout_sem.at[0], wout_sem.at[1], {"model": 0})
+
+    def heads_copy(c, peer):
+        slot = lax.rem(c, 2)
+        return remote(
+            at_st.at[pl.ds(pl.multiple_of(peer * tq, tq), tq)], heads_r.at[slot, me],
+            heads_sem.at[0], heads_sem.at[1 + slot], {"model": peer},
+        )
+
+    def heads_all(c):
+        slot = lax.rem(c, 2)
+        part = heads_r.at[slot, pl.ds(0, others)]
+        return remote(part, part, heads_sem.at[0], heads_sem.at[1 + slot], {"model": 0})
+
     def h_copy(c, m):
         return remote(
             hsend, hbuf.at[quarter(c, me)], h_ssem.at[0], h_rsem.at[c], {"stage": up_stage, "model": m}
@@ -288,9 +310,13 @@
             staged_out(0, c).wait()
             staged_out(2, c).wait()
 
-        @pl.when(c >= 2)
+        @pl.when((c >= 2) & jnp.logical_not(spread))
         def _():
             rs_drain(0, c)
+
+        @pl.when((c >= 1) & spread)
+        def _():
+            heads_all(c).wait_send()
 
         slot = lax.rem(c, 2)
 
@@ -311,19 +337,41 @@
 
         by_prefix(c, attend)
         staged_out(2, c).start()
-        tile = tile_of(d_model)
-        for j in range(d_model // tile):
-            cols = slice(j * tile, (j + 1) * tile)
-            rs_s[0, slot, :, cols] = dot_nn(at_st[...], wout[:, cols]).astype(BF16)
-        rs_start(0, c)
+
+        @pl.when(jnp.logical_not(spread))
+        def _():
+            tile = tile_of(d_model)
+            for j in range(d_model // tile):
+                cols = slice(j * tile, (j + 1) * tile)
+                rs_s[0, lax.rem(c, 2), :, cols] = dot_nn(at_st[...], wout[own_heads, cols]).astype(BF16)
+            rs_start(0, c)
+
+        @pl.when(spread)
+        def _():
+            for d in send_order:
+                heads_copy(c, lax.rem(me + d, n_model)).start()
+            heads_r[lax.rem(c, 2), me] = at_st[own, :]
 
     def fwd_mid(c, first):
         @pl.when(jnp.logical_not(first))
         def _():
             ag_drain(0, nbbuf)
 
-        mid = rs_sum(0, c) + hbuf[quarter(c, me), :].astype(F32)
-        midq[c] = mid
+        @pl.when(jnp.logical_not(spread))
+        def _():
+            midq[c] = rs_sum(0, c) + hbuf[quarter(c, me), :].astype(F32)
+
+        @pl.when(first & spread)
+        def _():
+            wout_all().wait_recv()
+
+        @pl.when(spread)
+        def _():
+            heads_all(c).wait_recv()
+            attn = jnp.concatenate([heads_r[lax.rem(c, 2), m] for m in range(n_model)], axis=-1)
+            midq[c] = dot_nn(attn, wout[...]) + hbuf[quarter(c, me), :].astype(F32)
+
+        mid = midq[c]
         nbbuf[quarter(c, me), :] = (mid * rms_inverse(mid) * gain_b).astype(BF16)
         ag_start(0, nbbuf, c)
 
@@ -407,7 +455,7 @@
         lax.fori_loop(0, n + deepest, body, 0)
 
     def flip_weights():
-        for w, w_t in ((wdown, wdown_t), (wup, wup_t), (wout, wout_t), (wqkv, wqkv_t)):
+        for w, w_t in ((wdown, wdown_t), (wup, wup_t), (wout.at[own_heads], wout_t), (wqkv, wqkv_t)):
             depth = tile_of(w.shape[0], 256)
             for r in range(w.shape[0] // depth):
                 w_t[:, r * depth : (r + 1) * depth] = w[r * depth : (r + 1) * depth, :].T
@@ -416,6 +464,12 @@
     def _():
         for k in range(slabs + 3):
             weight_copy(k).wait()
+
+        @pl.when(spread)
+        def _():
+            for d in send_order:
+                wout_copy(lax.rem(me + d, n_model)).start()
+
         flip_weights()
 
     pipeline(
@@ -430,8 +484,17 @@
     dkacc[...] = jnp.zeros_like(dkacc)
     dvacc[...] = jnp.zeros_like(dvacc)
 
+    @pl.when(jnp.logical_not(spread))
+    def _():
+        for c in range(min(n, 2)):
+            rs_drain(0, c)
+
+    @pl.when(spread)
+    def _():
+        heads_all(0).wait_send()
+        wout_all().wait_send()
+
     for c in range(min(n, 2)):
-        rs_drain(0, c)
         rs_drain(1, c)
     ag_drain(0, nbbuf)
     staged_out(0, 0).wait()
@@ -666,7 +729,7 @@
     vmem_spec = pl.BlockSpec(memory_space=pltpu.VMEM)
     scratch = [
         pltpu.VMEM((d_model, 3 * hw), BF16),
-        pltpu.VMEM((hw, d_model), BF16),
+        pltpu.VMEM((n_model * hw, d_model), BF16),
         pltpu.VMEM((d_model, ff), BF16),
         pltpu.VMEM((ff, d_model), BF16),
         pltpu.VMEM((3 * hw, d_model), BF16),
@@ -685,6 +748,7 @@
         pltpu.VMEM((seq, hw), F32),
         pltpu.VMEM((4, 2, near, tq, d_model), BF16),
         pltpu.VMEM((4, 2, t, d_model), BF16),
+        pltpu.VMEM((2, n_model, tq, hw), BF16),
         pltpu.VMEM((t, d_model), BF16),
         pltpu.VMEM((t, ff), BF16),
         pltpu.VMEM((t, hw), BF16),
@@ -711,6 +775,8 @@
         dma((4, 2)),
         dma((2, 2)),
         dma((2,)),
+        dma((2,)),
+        dma((3,)),
         dma((5,)),
         dma((3,)),
         dma((2,)),

time: 667 us -> 655 us (0.982)
  Pallas kernels: 666 us -> 654 us
    pallas_call x1, Pallas kernels: 645 us -> 633 us  [run_step(): pl.pallas_call(functools.partial(step_kernel, cfg), name='pipeline_step',...]
where the time goes in v5:
time: 655 us; the launch traced here: 654 us
  Pallas kernels  654 us (100%)
    pallas_call x1, Pallas kernels, run_step(): pl.pallas_call(functools.partial(step_kernel, cfg), name='pipeline_step',...  633 us
    pallas_call x1, Pallas kernels, weight_grads(): pl.pallas_call(functools.partial(grads_kernel, nj, bm), name='weight_grad...  21 us

profile of v5, /device:TPU:96, one launch (start us, length us, event | category | flops | bytes accessed | tf_op | source)
XLA Modules:
  0.0 654.5 jit_solution(3860491185659909988)
XLA Ops:
  0.6 632.7 %pipeline_step.1 = (bf16[1024,1536]{1,0:T(8,128)(2,1)}, bf16[1024,1536]{1,0:T(8,128)(2,1)}, bf16[1024,384]{1,0:T(8,128)(2,1)}, bf16[1024,1536]{1,0:T(8,128)(2,1)...) custom-call(bf16[1024,1536]{1,0:T(8,128)(2,1)} %bitcast.24, ...), custom_call_target="tpu_custom_call" | custom-call | tf_op jit(solution)/shard_map/pipeline_step/pallas_call | solution.py:786
  633.3 21.0 %weight_grads.1 = (f32[384,1536]{1,0:T(8,128)}, f32[1536,1536]{1,0:T(8,128)}, f32[1536,1536]{1,0:T(8,128)}, f32[9,1536,128]{2,1,0:T(8,128)}, f32[1,1]{1,0:T(1,128)}, /*index=5*/f32[2,1536]{1,0:T(2,128)}) custom-call(bf16[1024,384]{1,0:T(8,128)(2,1)} %get-tuple-element.21.refs_0_, bf16[1024,1536]{1,0:T(8,128)(2,1)} %get-tuple-element.22.refs_1_, ...), custom_call_target="tpu_custom_call" | custom-call | tf_op jit(solution)/shard_map/weight_grads/pallas_call | solution.py:875

commit v6 on v5

--- a/solution.py
+++ b/solution.py
@@ -12,7 +12,7 @@
 NEG_BIG = -1e30
 CHUNK = 64
 KEY_STEP = 256
-SPREAD_FROM = 4
+SPREAD_FROM = 3
 GRAD_ROWS = 768
 LOG2E = 1.4426950408889634
 F32 = jnp.float32
@@ -473,7 +473,7 @@
         flip_weights()
 
     pipeline(
-        [(fwd_attn, 0, "fwd_attn"), (fwd_end, 2, "fwd_end", lax.rem(stage, 2) == 0), (fwd_mlp, 1, "fwd_mlp"), (fwd_mid, 0, "fwd_mid"), (fwd_end, 1, "fwd_end", lax.rem(stage, 2) == 1)],
+        [(fwd_attn, 0, "fwd_attn"), (fwd_end, 2, "fwd_end", (lax.rem(stage, 2) == 0) | (stage >= SPREAD_FROM)), (fwd_mlp, 1, "fwd_mlp"), (fwd_mid, 0, "fwd_mid"), (fwd_end, 1, "fwd_end", jnp.logical_not((lax.rem(stage, 2) == 0) | (stage >= SPREAD_FROM)))],
         lambda j: j,
     )
 

time: 655 us -> 642 us (0.980)
  Pallas kernels: 654 us -> 641 us
    pallas_call x1, Pallas kernels: 633 us -> 620 us  [run_step(): pl.pallas_call(functools.partial(step_kernel, cfg), name='pipeline_step',...]
where the time goes in v6:
time: 642 us
  Pallas kernels  641 us (100%)
    pallas_call x1, Pallas kernels, run_step(): pl.pallas_call(functools.partial(step_kernel, cfg), name='pipeline_step',...  620 us
    pallas_call x1, Pallas kernels, weight_grads(): pl.pallas_call(functools.partial(grads_kernel, nj, bm), name='weight_grad...  21 us

profile of v6, /device:TPU:96, one launch (start us, length us, event | category | flops | bytes accessed | tf_op | source)
XLA Modules:
  0.0 642.2 jit_solution(17088951198540568051)
XLA Ops:
  0.6 620.4 %pipeline_step.1 = (bf16[1024,1536]{1,0:T(8,128)(2,1)}, bf16[1024,1536]{1,0:T(8,128)(2,1)}, bf16[1024,384]{1,0:T(8,128)(2,1)}, bf16[1024,1536]{1,0:T(8,128)(2,1)...) custom-call(bf16[1024,1536]{1,0:T(8,128)(2,1)} %bitcast.24, ...), custom_call_target="tpu_custom_call" | custom-call | tf_op jit(solution)/shard_map/pipeline_step/pallas_call | solution.py:786
  621.1 21.0 %weight_grads.1 = (f32[384,1536]{1,0:T(8,128)}, f32[1536,1536]{1,0:T(8,128)}, f32[1536,1536]{1,0:T(8,128)}, f32[9,1536,128]{2,1,0:T(8,128)}, f32[1,1]{1,0:T(1,128)}, /*index=5*/f32[2,1536]{1,0:T(2,128)}) custom-call(bf16[1024,384]{1,0:T(8,128)(2,1)} %get-tuple-element.21.refs_0_, bf16[1024,1536]{1,0:T(8,128)(2,1)} %get-tuple-element.22.refs_1_, ...), custom_call_target="tpu_custom_call" | custom-call | tf_op jit(solution)/shard_map/weight_grads/pallas_call | solution.py:875
